TPU v7x, 256 devices: a whole 4x4x8 slice. The times are simulated.
256 devices in a mesh: dp: 128 (over y, x_lo, z, core), rep: 2 (over x_hi).
Axes of the slice: x: 4 (x_hi: 2, x_lo: 2; x = x_hi * 2 + x_lo), y: 4, z: 8, core: 2. Of those that a mesh axis runs over, the one named last changes fastest.
Arguments:
- q_hidden: bfloat16 [2, 128, 128, 768], P('rep', 'dp'), may hold values from -8 to 8
- p_hidden: bfloat16 [2, 128, 128, 768], P('rep', 'dp'), may hold values from -8 to 8
- w_up: bfloat16 [1536, 768], replicated, may hold values from -0.21875 to 0.21875
- w_down: bfloat16 [1536, 768], replicated, may hold values from -0.15625 to 0.15625
- pos_index: int32 [2, 128], P('rep', 'dp'), may hold values from 0 to 127
- hard_index: int32 [2, 128, 2], P('rep', 'dp'), may hold values from 0 to 127
Outputs:
- w_up_grad: float32 [1536, 768], P(('dp', 'rep'))
- mean_loss: float32 [], replicated
All inputs are finite; a program needn't handle non-finite values.
Results may differ from a plain program's by a relative error of at most 0.008.
Values may be sent and summed in bfloat16 or wider, within the bound.
No kernel may reach another device: no remote copies, remote signals or barrier semaphores. Data moves between devices by JAX's collectives and lax.ppermute only.
A program may use at most 64 MiB of HBM per device.

v0:
```python
import math

import jax
import jax.numpy as jnp
from jax import lax
from jax.sharding import Mesh
from jax.sharding import PartitionSpec as P

DP = ("dp_0", "dp_1", "dp_2", "dp_3")
DP_REP = ("dp_0", "dp_1", "dp_2", "dp_3", "rep")


norm_eps = 1e-06
HARD_BOOST = 1.5


def from_everyone(shard, axis):
    copies = jnp.broadcast_to(shard, (lax.axis_size(axis), *shard.shape))
    return lax.all_to_all(copies, axis, split_axis=0, concat_axis=0, tiled=True)


def joined_along(tiles, dim):
    dims = list(tiles.shape[1:])
    dims[dim] *= tiles.shape[0]
    return jnp.moveaxis(tiles, 0, dim).reshape(dims)


def gather_axes(shard, axes, dim):
    far, near = axes
    tiles = from_everyone(from_everyone(shard, far), near)
    return joined_along(tiles.swapaxes(0, 1).reshape(-1, *shard.shape), dim)


def sent_together(arrays, axis, dim, along):
    columns = [a.reshape(*a.shape[:along], -1) for a in arrays]
    both = jnp.concatenate(columns, axis=along)
    out, at, done = (lax.all_gather(both, axis, axis=dim, tiled=True), 0, [])
    for a, column in zip(arrays, columns):
        section = out[..., at : at + column.shape[along]]
        done.append(section.reshape(*section.shape[:along], *a.shape[along:]))
        at += column.shape[along]
    return tuple(done)


def one_axis_at_a_time(shard, axes):
    for axis in axes:
        shard = lax.psum(shard, axis)
    return shard


def in_blocks(shard, dim, count):
    before, after = (shard.shape[:dim], shard.shape[dim + 1 :])
    return jnp.moveaxis(shard.reshape(*before, count, -1, *after), dim, 0)


def own_tiles(shard, axis, dim):
    count = lax.axis_size(axis)
    tiles = in_blocks(shard, dim, count)
    length = shard.size // count
    spare = max(2048 - length, -length % 1024)
    padded = jnp.pad(tiles.reshape(count, length), ((0, 0), (0, spare)))
    own = lax.psum_scatter(padded.reshape(-1, 128), axis, scatter_dimension=0, tiled=True)
    return own.reshape(-1)[:length].reshape(tiles.shape[1:])


def gelu_slope(values):
    cdf_part = 0.5 * (1.0 + lax.erf(values * (1.0 / math.sqrt(2.0))))
    return cdf_part + values * jnp.exp(-0.5 * values * values) * (1.0 / math.sqrt(2.0 * math.pi))


def contract_rows(left, right):
    return lax.dot_general(
        left, right, (((0,), (0,)), ((), ())), preferred_element_type=jnp.float32
    )


def shards(q_hidden, p_hidden, w_up, w_down, pos_index, hard_index):
    pair_count = q_hidden.shape[1]
    length = q_hidden.shape[2]
    features = q_hidden.shape[3]
    pool_size = pair_count * lax.axis_size(DP)
    tokens = jnp.concatenate([q_hidden[0], p_hidden[0]], 0).reshape(-1, features)
    pre_act = lax.dot_general(
        tokens, w_up, (((1,), (1,)), ((), ())), preferred_element_type=jnp.float32
    )
    hidden = jax.nn.gelu(pre_act, approximate=False).astype(jnp.bfloat16)
    summed = tokens.astype(jnp.float32) + jnp.dot(
        hidden, w_down, preferred_element_type=jnp.float32
    )
    row_mean = jnp.mean(summed, -1, keepdims=True)
    centred = summed - row_mean
    inv_scale = lax.rsqrt(jnp.mean(centred * centred, -1, keepdims=True) + norm_eps)
    normed = centred * inv_scale
    embedded = jnp.mean(normed.reshape(2 * pair_count, length, features), 1).astype(jnp.bfloat16)
    query_embed = embedded[:pair_count]
    passage_embed = embedded[pair_count:]
    all_passages = gather_axes(passage_embed, (("dp_0", "dp_1", "dp_2"), "dp_3"), 0)
    columns = jnp.arange(pool_size, dtype=jnp.int32)
    all_queries = gather_axes(query_embed, (("dp_0", "dp_1", "dp_2"), "dp_3"), 0)
    all_targets, all_negatives = sent_together((pos_index[0], hard_index[0]), DP, 0, 1)
    scores = lax.dot_general(
        all_queries, all_passages, (((1,), (1,)), ((), ())), preferred_element_type=jnp.float32
    )
    hard_mask = jnp.any(all_negatives[:, :, None] == columns, axis=1)
    logits = scores + HARD_BOOST * hard_mask.astype(jnp.float32)
    row_max = jnp.max(logits, -1, keepdims=True)
    log_total = row_max + jnp.log(jnp.sum(jnp.exp(logits - row_max), -1, keepdims=True))
    target = all_targets[:, None] == columns
    picked = jnp.sum(jnp.where(target, logits, 0.0), -1)
    weights = (jnp.exp(logits - log_total) - target.astype(jnp.float32)).astype(jnp.bfloat16)
    losses, weights = (log_total[:, 0] - picked, weights)
    first_row = lax.axis_index(DP) * pair_count
    own_losses = lax.dynamic_slice_in_dim(losses, first_row, pair_count, 0)
    own_rows = lax.dynamic_slice_in_dim(weights, first_row, pair_count, 0)
    own_columns = lax.dynamic_slice_in_dim(weights, first_row, pair_count, 1)
    d_query = jnp.dot(own_rows, all_passages, preferred_element_type=jnp.float32)
    d_passage = contract_rows(own_columns, all_queries)
    loss_sum = one_axis_at_a_time(jnp.sum(own_losses), DP_REP)
    mean_loss = loss_sum / (pool_size * lax.axis_size("rep"))
    d_embed = jnp.concatenate([d_query, d_passage], 0)
    grad_out = jnp.repeat(d_embed / length, length, axis=0)
    grad_resid = inv_scale * (
        grad_out
        - jnp.mean(grad_out, -1, keepdims=True)
        - normed * jnp.mean(grad_out * normed, -1, keepdims=True)
    )
    grad_low = grad_resid.astype(jnp.bfloat16)
    grad_hidden = lax.dot_general(
        grad_low, w_down, (((1,), (1,)), ((), ())), preferred_element_type=jnp.float32
    )
    grad_pre = (grad_hidden * gelu_slope(pre_act)).astype(jnp.bfloat16)
    up_terms = contract_rows(grad_pre, tokens)
    w_up_grad = own_tiles(up_terms, DP_REP, 0)
    return (w_up_grad, mean_loss)


def solution(mesh):
    finer = Mesh(
        mesh.devices.reshape(4, 2, 8, 2, mesh.shape["rep"]), ("dp_0", "dp_1", "dp_2", "dp_3", "rep")
    )
    return jax.shard_map(
        shards,
        mesh=finer,
        in_specs=(
            P("rep", DP, None, None),
            P("rep", DP, None, None),
            P(),
            P(),
            P("rep", DP),
            P("rep", DP, None),
        ),
        out_specs=(P(DP_REP, None), P()),
        check_vma=False,
    )
```

profile of v0, /device:TPU:8, one launch (start us, length us, event | category | flops | bytes accessed | tf_op | source)
XLA Modules:
  0.0 539.6 jit_solution(12899937329911014059)
XLA Ops:
  7.2 1.2 pad_maximum_fusion
  8.4 2.5 fusion.100
  10.9 4.1 fusion.98
  15.8 0.8 broadcast_in_dim.14
  16.6 0.5 broadcast.114
  17.1 2.7 reduce.11
  19.8 1.6 reshape.93
  21.4 13.2 %all-to-all-start.2 = ((bf16[64,2,384]{2,1,0:T(2,128)(2,1)}), bf16[64,2,384]{2,1,0:T(2,128)(2,1)}, u32[]{:S(2)}, u32[]{:S(2)}) async-start(bf16[64,2,384]{2,1,0:T(2,128)(2,1)} %reshape.93), calls=%async_computation.2 | async-start | bytes 196608 | tf_op jit(solution)/shard_map/all_to_all | solution.py:19
  35.4 135.1 %all-gather = s32[128,1,3]{2,1,0:T(1,128)S(1)} all-gather(s32[1,1,3]{2,1,0:T(1,128)S(1)} %add_bitcast_fusion), channel_id=1, replica_groups=mesh['dp_0'=4,'dp_1'=2,'dp_2'=8,'dp_3'=2,'rep'=2] {'dp_0','dp_1','dp_2',..., dimensions={0}, use_global_device_ids=true | all-gather | bytes 1548 | tf_op jit(solution)/shard_map/all_gather | solution.py:37
  170.4 0.6 copy-done.2
  171.1 0.7 slice.29
  171.8 0.9 copy.12
  172.7 0.8 broadcast_in_dim.11
  173.4 2.7 reduce.10
  176.2 1.6 reshape.91
  177.7 1.6 reshape.94
  179.4 0.9 copy.18
  180.3 4.6 all_to_all.26
  184.9 27.2 %all-to-all-start = ((bf16[64,2,384]{2,1,0:T(2,128)(2,1)}), bf16[64,2,384]{2,1,0:T(2,128)(2,1)}, u32[]{:S(2)}, u32[]{:S(2)}) async-start(bf16[64,2,384]{2,1,0:T(2,128)(2,1)} %reshape.91), calls=%async_computation | async-start | bytes 196608 | tf_op jit(solution)/shard_map/all_to_all | solution.py:19
  212.4 1.5 slice_reduce_fusion
  213.9 1.8 copy.11
  215.7 1.7 reshape_reshape.10
  217.4 4.3 all-to-all-done
  221.7 1.6 reshape.92
  223.3 0.9 copy.19
  224.3 3.9 all_to_all.27
  228.2 0.9 copy.10
  229.0 1.7 reshape_reshape.9
  230.7 1.3 fusion.99
  232.0 0.7 select_reduce_fusion
  232.7 0.7 subtract_convert_fusion
  233.4 1.1 fusion.58
  234.6 1.1 fusion.56
  235.9 0.9 fusion.19
  236.9 1.0 fusion.18
  237.9 5.4 fusion.15
  243.3 5.5 %reshape_reshape.11 = f32[256,4608]{1,0:T(8,128)} reshape(f32[1536,768]{1,0:T(8,128)} %fusion.15) | data formatting | bytes 9437184 | tf_op jit(solution)/shard_map/reshape;reshape | solution.py:61
  248.8 5.3 pad.4
  254.1 6.3 %reshape.76 = f32[10240,128]{1,0:T(8,128)} reshape(f32[256,5120]{1,0:T(8,128)} %pad.4) | data formatting | bytes 10485760 | tf_op jit(solution)/shard_map/reshape | solution.py:62
  260.4 0.6 dynamic_slice.11
  261.0 10.4 %psum.35 = f32[]{:T(128)} all-reduce(f32[]{:T(128)} %bitcast.12), channel_id=1, replica_groups=mesh['dp_0'=4,'dp_1'=2,'dp_2'=8,'dp_3'=2,'rep'=2] {'dp_0'}, use_global_device_ids=true, to_apply=%region_10.11 | all-reduce | flops 1 | bytes 8 | tf_op jit(solution)/shard_map/psum | solution.py:47
  271.4 5.5 %psum.36 = f32[]{:T(128)} all-reduce(f32[]{:T(128)} %psum.35), channel_id=1, replica_groups=mesh['dp_0'=4,'dp_1'=2,'dp_2'=8,'dp_3'=2,'rep'=2] {'dp_1'}, use_global_device_ids=true, to_apply=%region_11.12 | all-reduce | flops 1 | bytes 8 | tf_op jit(solution)/shard_map/psum | solution.py:47
  276.9 15.6 %psum.37 = f32[]{:T(128)} all-reduce(f32[]{:T(128)} %psum.36), channel_id=1, replica_groups=mesh['dp_0'=4,'dp_1'=2,'dp_2'=8,'dp_3'=2,'rep'=2] {'dp_2'}, use_global_device_ids=true, to_apply=%region_12.13 | all-reduce | flops 1 | bytes 8 | tf_op jit(solution)/shard_map/psum | solution.py:47
  292.5 3.1 psum.38
  295.6 7.0 %psum.39 = f32[]{:T(128)} all-reduce(f32[]{:T(128)} %psum.38), channel_id=1, replica_groups=mesh['dp_0'=4,'dp_1'=2,'dp_2'=8,'dp_3'=2,'rep'=2] {'rep'}, use_global_device_ids=true, to_apply=%region_14.15 | all-reduce | flops 1 | bytes 8 | tf_op jit(solution)/shard_map/psum | solution.py:47
  303.3 227.0 %all-reduce.4.cloned.1.call-done = f32[10240,128]{1,0:T(8,128)} async-done(((f32[10240,128]{1,0:T(8,128)}), f32[10240,128]{1,0:T(8,128)}) %all-reduce.4.cloned.1.call-update) | async-done | bytes 5242896
  530.3 0.7 constant_dynamic-slice_fusion
  531.0 0.6 reshape.77
  (35 shorter events, 1.6 us)
Async XLA Ops:
  7.2 3.7 copy-start
  10.9 4.1 copy-start.1
  15.0 20.3 %copy-start.7 = (s32[1,1,2]{2,1,0:T(1,128)S(1)}, s32[1,1,2]{2,1,0:T(1,128)}, u32[]{:S(2)}) copy-start(s32[1,1,2]{2,1,0:T(1,128)} %param.11) | copy-start | bytes 28
  15.0 0.5 copy-start.3
  15.2 0.6 copy-start.5
  21.4 156.3 %all-to-all-start.2 = ((bf16[64,2,384]{2,1,0:T(2,128)(2,1)}), bf16[64,2,384]{2,1,0:T(2,128)(2,1)}, u32[]{:S(2)}, u32[]{:S(2)}) async-start(bf16[64,2,384]{2,1,0:T(2,128)(2,1)} %reshape.93), calls=%async_computation.2 | async-start | bytes 196608 | tf_op jit(solution)/shard_map/all_to_all | solution.py:19
  170.4 0.6 copy-start.2
  184.9 36.7 %all-to-all-start = ((bf16[64,2,384]{2,1,0:T(2,128)(2,1)}), bf16[64,2,384]{2,1,0:T(2,128)(2,1)}, u32[]{:S(2)}, u32[]{:S(2)}) async-start(bf16[64,2,384]{2,1,0:T(2,128)(2,1)} %reshape.91), calls=%async_computation | async-start | bytes 196608 | tf_op jit(solution)/shard_map/all_to_all | solution.py:19
  212.2 318.1 %all-reduce.4.cloned.1.call-start = ((), (), s32[]{:S(2)}) async-start(), calls=%async_computation.4 | async-start | bytes 10485760
  230.7 6.2 %copy-start.4 = (f32[256]{0:T(256)S(1)}, f32[256]{0:T(256)}, u32[]{:S(2)}) copy-start(f32[256]{0:T(256)} %copy-done.3) | copy-start | bytes 3076
  230.7 6.2 %copy-start.6 = (f32[256]{0:T(256)S(1)}, f32[256]{0:T(256)}, u32[]{:S(2)}) copy-start(f32[256]{0:T(256)} %copy-done.5) | copy-start | bytes 3076
Sparse Core Ops, SparseCore 0:
  260.6 269.6 all-reduce.3
where the time goes:
time: 541 us; the launch traced here: 540 us
  waiting for transfers between devices  231 us (43%)
  blocking collectives  185 us (34%)
  starting transfers between devices  40.5 us (7%)
  local copies, waits for them, and re-layouts  40 us (7%)
  between operations  16.7 us (3%)
  matrix products  15.3 us (3%)
  other arithmetic  10.8 us (2%)
    unnamed x2, waiting for transfers between devices  227 us
    all_gather x1, blocking collectives, sent_together(): out, at, done = (lax.all_gather(both, axis, axis=dim, tiled=True), 0, [])  135 us
    psum x5, blocking collectives, one_axis_at_a_time(): shard = lax.psum(shard, axis)  41.6 us
    all_to_all x2, starting transfers between devices, from_everyone(): return lax.all_to_all(copies, axis, split_axis=0, concat_axis=0, tiled=True)  40.4 us
  transfers between devices with their start and end apart: 3, of which 2 were waited for; matrix products, arithmetic and copies ran while one was open for 2% of the time, Pallas kernels for 0%

commit v1 on v0

v1 whole, which is shorter than its diff:
```python
import functools
import math

import jax
import jax.numpy as jnp
from jax import lax
from jax.experimental import pallas as pl
from jax.experimental.pallas import tpu as pltpu
from jax.sharding import Mesh
from jax.sharding import PartitionSpec as P

DP = ("y", "xl", "z", "c")
SWAP = ((0, 1), (1, 0))

norm_eps = 1e-06
HARD_BOOST = 1.5
SQRT_HALF = 1.0 / math.sqrt(2.0)
DENSITY = 1.0 / math.sqrt(2.0 * math.pi)
BF = jnp.bfloat16
F32 = jnp.float32
MIB = 1 << 20

WHOLE = pl.BlockSpec(memory_space=pltpu.VMEM)
SCALARS = pl.BlockSpec(memory_space=pltpu.SMEM)
ANYWHERE = pl.BlockSpec(memory_space=pl.ANY)

SPAN = 16


def rows_by_rows(left, right):
    return lax.dot_general(left, right, (((1,), (1,)), ((), ())), preferred_element_type=F32)


def call(body, outs, ins, scratch=(), vmem=24):
    return pl.pallas_call(
        body,
        out_shape=outs,
        in_specs=ins,
        out_specs=jax.tree.map(lambda _: WHOLE, outs),
        scratch_shapes=scratch,
        compiler_params=pltpu.CompilerParams(vmem_limit_bytes=vmem * MIB),
    )


def encode_body(chunk, pos, hard, q, p, wu_hbm, wd_hbm, message, normed_out, inv_out, wu, wd, sem_u, sem_d):
    hidden_units, features = wu.shape
    steps = hidden_units // chunk

    def copies(n):
        at = pl.ds(n * chunk, chunk)
        return (
            pltpu.make_async_copy(wu_hbm.at[at], wu.at[at], sem_u.at[n]),
            pltpu.make_async_copy(wd_hbm.at[at], wd.at[at], sem_d.at[n]),
        )

    for n in range(steps):
        for copy in copies(n):
            copy.start()
    tokens = jnp.concatenate([q[...], p[...]], 0)
    summed = tokens.astype(F32)
    for n in range(steps):
        at = pl.ds(n * chunk, chunk)
        up, down = copies(n)
        up.wait()
        pre_act = rows_by_rows(tokens, wu[at, :])
        hidden = (0.5 * pre_act * (1.0 + lax.erf(pre_act * SQRT_HALF))).astype(BF)
        down.wait()
        summed = summed + jnp.dot(hidden, wd[at, :], preferred_element_type=F32)
    row_mean = jnp.mean(summed, -1, keepdims=True)
    centred = summed - row_mean
    inv_scale = lax.rsqrt(jnp.mean(centred * centred, -1, keepdims=True) + norm_eps)
    normed = centred * inv_scale
    normed_out[...] = normed.astype(BF)
    inv_out[...] = jnp.transpose(jnp.broadcast_to(inv_scale, (inv_scale.shape[0], 128)))[:8]
    length = q.shape[0]
    rows = []
    for s in range(2):
        embed = jnp.mean(normed[s * length : (s + 1) * length], 0, keepdims=True)
        rows += [embed[:, k * 128 : (k + 1) * 128] for k in range(features // 128)]
    lane = lax.broadcasted_iota(jnp.int32, (1, 128), 1)
    index_row = jnp.where(lane == 0, pos[0, 0], jnp.where(lane == 1, hard[0, 0], hard[0, 1]))
    rows.append(index_row.astype(F32))
    rows.append(jnp.zeros((SPAN - len(rows), 128), F32))
    block = jnp.concatenate(rows, 0).astype(BF)
    message[...] = jnp.broadcast_to(block[None], message.shape)


def encode(pos, hard, q, p, w_up, w_down, peers):
    length, features = q.shape
    hidden_units = w_up.shape[0]
    chunk = 256
    steps = hidden_units // chunk
    return call(
        functools.partial(encode_body, chunk),
        (
            jax.ShapeDtypeStruct((peers, SPAN, 128), BF),
            jax.ShapeDtypeStruct((2 * length, features), BF),
            jax.ShapeDtypeStruct((8, 2 * length), F32),
        ),
        [SCALARS, SCALARS, WHOLE, WHOLE, ANYWHERE, ANYWHERE],
        [
            pltpu.VMEM((hidden_units, features), BF),
            pltpu.VMEM((hidden_units, features), BF),
            pltpu.SemaphoreType.DMA((steps,)),
            pltpu.SemaphoreType.DMA((steps,)),
        ],
    )(pos, hard, q, p, w_up, w_down)


def prepare_body(blocks, q, p, qs, ps, normed, normed_s, inv, inv_s, wu, wd, slope_out, along_out, wd_out, wu_mine):
    core = lax.axis_index("c")
    features = wu.shape[1]
    width = wu.shape[0] // blocks
    half = width // 2
    mine = lax.broadcasted_iota(jnp.int32, (half, width), 0)
    source = lax.broadcasted_iota(jnp.int32, (half, width), 1)
    run = half // 8
    skipped = sum((mine >= run * k).astype(jnp.int32) for k in range(1, 8))
    pick = (source == mine + run * (skipped + core)).astype(F32).astype(BF)
    for b in range(blocks):
        old, new = pl.ds(b * width, width), pl.ds(b * half, half)
        wu_mine[new, :] = jnp.dot(pick, wu[old, :], preferred_element_type=F32).astype(BF)
        wd_out[new, :] = jnp.dot(pick, wd[old, :], preferred_element_type=F32).astype(BF)
    tokens = jnp.concatenate([q[...], p[...], qs[...], ps[...]], 0)
    normed_all = jnp.concatenate([normed[...], normed_s[...]], 0)
    inv_all = jnp.concatenate([inv[0:1, :], inv_s[0:1, :]], 1)
    chunk = 256
    for n in range(wu_mine.shape[0] // chunk):
        at = pl.ds(n * chunk, chunk)
        pre_act = rows_by_rows(wu_mine[at, :], tokens)
        slope = 0.5 * (1.0 + lax.erf(pre_act * SQRT_HALF))
        slope = slope + pre_act * jnp.exp(-0.5 * pre_act * pre_act) * DENSITY
        scaled = slope * inv_all
        slope_out[at, :] = scaled.astype(BF)
        along_out[at, :] = (scaled * rows_by_rows(wd_out[at, :], normed_all)).astype(BF)


def prepare(blocks, q, p, qs, ps, normed, normed_s, inv, inv_s, w_up, w_down):
    hidden_units, features = w_up.shape
    half, count = hidden_units // 2, 4 * q.shape[0]
    return call(
        functools.partial(prepare_body, blocks),
        (
            jax.ShapeDtypeStruct((half, count), BF),
            jax.ShapeDtypeStruct((half, count), BF),
            jax.ShapeDtypeStruct((half, features), BF),
        ),
        [WHOLE] * 10,
        [pltpu.VMEM((half, features), BF)],
        vmem=28,
    )(q, p, qs, ps, normed, normed_s, inv, inv_s, w_up, w_down)


def gradient_body(gathered, slope, along, wd, q, p, qs, ps, normed, normed_s, terms, loss, wide, d_query, d_passage):
    core = lax.axis_index("c")
    place = (lax.axis_index("y") * 2 + lax.axis_index("xl")) * 8 + lax.axis_index("z")
    pool, features = d_query.shape
    cores_apart = pool // 2
    length = q.shape[0]
    wide[...] = gathered[...].astype(F32)
    parts = features // 128
    from_all = lambda k: wide[pl.ds(k, pool, stride=SPAN), :]
    queries = jnp.concatenate([from_all(k) for k in range(parts)], 1).astype(BF)
    passages = jnp.concatenate([from_all(parts + k) for k in range(parts)], 1).astype(BF)
    indices = from_all(2 * parts)
    lane = lax.broadcasted_iota(jnp.int32, (1, pool), 1)
    late = (lane >= cores_apart).astype(jnp.int32)
    column = (2 * (lane - cores_apart * late) + late).astype(F32)
    target = indices[:, 0:1] == column
    named = (indices[:, 1:2] == column) | (indices[:, 2:3] == column)
    logits = rows_by_rows(queries, passages) + jnp.where(named, HARD_BOOST, 0.0)
    row_max = jnp.max(logits, -1, keepdims=True)
    log_total = row_max + jnp.log(jnp.sum(jnp.exp(logits - row_max), -1, keepdims=True))
    picked = jnp.sum(jnp.where(target, logits, 0.0), -1, keepdims=True)
    loss[...] = jnp.broadcast_to(jnp.sum(log_total - picked, 0, keepdims=True), loss.shape)
    weights = (jnp.exp(logits - log_total) - jnp.where(target, 1.0, 0.0)).astype(BF)
    d_query[...] = jnp.dot(weights, passages, preferred_element_type=F32)
    d_passage[...] = lax.dot_general(
        weights, queries, (((0,), (0,)), ((), ())), preferred_element_type=F32
    )
    own = core * cores_apart + place
    sibling = (1 - core) * cores_apart + place
    grad = jnp.concatenate(
        [d[pl.ds(at, 1), :] for at in (own, sibling) for d in (d_query, d_passage)], 0
    ) * (1.0 / length)
    level = grad - jnp.mean(grad, -1, keepdims=True)
    both = jnp.concatenate([grad, level], 0)
    high = both.astype(BF)
    low = (both - high.astype(F32)).astype(BF)
    vectors = jnp.concatenate([high, low], 0)
    normed_all = jnp.concatenate([normed[...], normed_s[...]], 0)
    shares = rows_by_rows(vectors, normed_all)
    offsets = rows_by_rows(wd[...], vectors)
    pieces = []
    for s in range(4):
        at = slice(s * length, (s + 1) * length)
        share = (shares[s : s + 1, at] + shares[8 + s : 9 + s, at]) * (1.0 / features)
        offset = offsets[:, 4 + s : 5 + s] + offsets[:, 12 + s : 13 + s]
        piece = offset * slope[:, at].astype(F32) - share * along[:, at].astype(F32)
        pieces.append(piece.astype(BF))
    grad_pre = jnp.concatenate(pieces, 1)
    tokens = jnp.concatenate([q[...], p[...], qs[...], ps[...]], 0)
    terms[...] = jnp.dot(grad_pre, tokens, preferred_element_type=F32).astype(BF)


def gradient(gathered, slope, along, wd, q, p, qs, ps, normed, normed_s):
    half, features = wd.shape
    pool = gathered.shape[0] // SPAN
    return call(
        gradient_body,
        (jax.ShapeDtypeStruct((half, features), BF), jax.ShapeDtypeStruct((8, 128), F32)),
        [WHOLE] * 10,
        [
            pltpu.VMEM(gathered.shape, F32),
            pltpu.VMEM((pool, features), F32),
            pltpu.VMEM((pool, features), F32),
        ],
    )(gathered, slope, along, wd, q, p, qs, ps, normed, normed_s)


def add_near_body(own_rows, arrived, loss, out):
    senders, rows, features = arrived.shape
    total = arrived[0].astype(F32)
    for s in range(1, senders):
        total = total + arrived[s].astype(F32)
    groups = rows // own_rows
    spread = lax.broadcasted_iota(jnp.int32, (groups * 8, rows), 0)
    source = lax.broadcasted_iota(jnp.int32, (groups * 8, rows), 1)
    group = spread >> 3
    inner = spread & 7
    pick = ((inner < own_rows) & (source == own_rows * group + inner)).astype(F32).astype(BF)
    placed = jnp.dot(pick, total.astype(BF), preferred_element_type=F32)
    value = loss[0:1, 0:1]
    first = value.astype(BF).astype(F32)
    second = (value - first).astype(BF).astype(F32)
    third = value - first - second
    lane = lax.broadcasted_iota(jnp.int32, (1, features), 1)
    split = jnp.where(lane == 0, first, jnp.where(lane == 1, second, jnp.where(lane == 2, third, 0.0)))
    is_loss = (lax.broadcasted_iota(jnp.int32, (groups * 8, 1), 0) & 7) == own_rows
    out[...] = jnp.where(is_loss, split, placed).astype(BF)


def add_near(arrived, loss, own_rows):
    groups = arrived.shape[1] // own_rows
    return call(
        functools.partial(add_near_body, own_rows),
        jax.ShapeDtypeStruct((groups * 8, arrived.shape[2]), BF),
        [WHOLE] * 2,
    )(arrived, loss)


def add_far_body(count, arrived, rows, mean_loss):
    total = arrived[0].astype(F32)
    for s in range(1, arrived.shape[0]):
        total = total + arrived[s].astype(F32)
    own = rows.shape[0]
    rows[...] = total[:own]
    loss = arrived[0, own : own + 1, 0:128].astype(F32) + arrived[1, own : own + 1, 0:128].astype(F32)
    lane = lax.broadcasted_iota(jnp.int32, (1, 128), 1)
    mean_loss[...] = jnp.sum(jnp.where(lane < 3, loss, 0.0), -1, keepdims=True) * (1.0 / count)


def add_far(arrived, own_rows, count):
    return call(
        functools.partial(add_far_body, count),
        (
            jax.ShapeDtypeStruct((own_rows, arrived.shape[2]), F32),
            jax.ShapeDtypeStruct((1, 1), F32),
        ),
        [WHOLE],
    )(arrived)


def exchange(tiles, axes):
    return lax.all_to_all(tiles, axes, split_axis=0, concat_axis=0, tiled=True)


def shards(q_hidden, p_hidden, w_up, w_down, pos_index, hard_index):
    features = w_up.shape[1]
    q = q_hidden.reshape(-1, features)
    p = p_hidden.reshape(-1, features)
    near, far = ("y", "xl"), ("z", "xh")
    near_count = lax.axis_size(near)
    far_count = lax.axis_size(far)
    own_rows = w_up.shape[0] // (2 * near_count * far_count)
    peers = lax.axis_size(("y", "xl", "z"))
    qs, ps = (lax.ppermute(a, "c", SWAP) for a in (q, p))
    message, normed, inv = encode(pos_index, hard_index.reshape(1, -1), q, p, w_up, w_down, peers)
    gathered = exchange(message, ("y", "xl", "z"))
    normed_s, inv_s = (lax.ppermute(a, "c", SWAP) for a in (normed, inv))
    slope, along, wd = prepare(near_count, q, p, qs, ps, normed, normed_s, inv, inv_s, w_up, w_down)
    gathered = lax.all_gather(gathered, "c", axis=0, tiled=True)
    terms, loss = gradient(
        gathered.reshape(-1, 128), slope, along, wd, q, p, qs, ps, normed, normed_s
    )
    arrived = exchange(terms.reshape(near_count, -1, features), near)
    partial = add_near(arrived, loss, own_rows)
    arrived = exchange(partial.reshape(far_count, 8, features), far)
    count = lax.axis_size(DP) * lax.axis_size("xh")
    rows, mean_loss = add_far(arrived, own_rows, count)
    return rows, mean_loss.reshape(())


def solution(mesh):
    finer = Mesh(mesh.devices.reshape(4, 2, 8, 2, mesh.shape["rep"]), ("y", "xl", "z", "c", "xh"))
    return jax.shard_map(
        shards,
        mesh=finer,
        in_specs=(
            P("xh", DP, None, None),
            P("xh", DP, None, None),
            P(),
            P(),
            P("xh", DP),
            P("xh", DP, None),
        ),
        out_specs=(P((*DP, "xh"), None), P()),
        check_vma=False,
    )
```

time: 541 us -> 92 us (0.17)
  waiting for transfers between devices: 231 us -> 2.57 us
  blocking collectives: 185 us -> 43.3 us
  starting transfers between devices: 40.5 us -> 14.3 us
  local copies, waits for them, and re-layouts: 40 us -> 15.9 us
  between operations: 16.7 us -> 1.39 us
  matrix products: 15.3 us -> 0 us
  Pallas kernels: 0 us -> 13.9 us
  other arithmetic: 10.8 us -> 0 us
    unnamed x2 -> x0, waiting for transfers between devices: 227 us -> none
    all_gather x1, blocking collectives: 135 us -> 2.51 us  [shards(): gathered = lax.all_gather(gathered, 'c', axis=0, tiled=True)]
    psum x5 -> x0, blocking collectives: 41.6 us -> none  [one_axis_at_a_time(): shard = lax.psum(shard, axis)]
    all_to_all x2, blocking collectives: 8.48 us -> 40.8 us  [exchange(): return lax.all_to_all(tiles, axes, split_axis=0, concat_axis=0, tiled=True)]
    all_to_all x2 -> x1, starting transfers between devices: 40.4 us -> 13.2 us  [exchange(): return lax.all_to_all(tiles, axes, split_axis=0, concat_axis=0, tiled=True)]
    dot_general x6 -> x0, matrix products: 15.3 us -> none  [the longest x2 6.43 us: contract_rows(): lax.dot_general(left, right, (((0,), (0,)), ((), ())), preferred_element_...]
    pallas_call x0 -> x5, Pallas kernels: none -> 13.9 us  [the longest x1 7.84 us: encode(): call(functools.partial(encode_body, chunk), (jax.ShapeDtypeStruct((peers,...]
    another operation x3 -> x0, local copies, waits for them, and re-layouts: 8.89 us -> none  [the longest x1 5.55 us: own_tiles(): padded = jnp.pad(tiles.reshape(count, length), ((0, 0), (0, spare)))]
  transfers between devices with their start and end apart: 3 -> 5, of which waited for: 2 -> 2; matrix products, arithmetic and copies ran while one was open for 2% -> 0% of each run, Pallas kernels for 0% -> 2%
where the time goes in v1:
time: 92 us; the launch traced here: 91.5 us
  blocking collectives  43.3 us (47%)
  local copies, waits for them, and re-layouts  15.9 us (17%)
  starting transfers between devices  14.3 us (16%)
  Pallas kernels  13.9 us (15%)
  waiting for transfers between devices  2.57 us (3%)
  between operations  1.39 us (2%)
    all_to_all x2, blocking collectives, exchange(): return lax.all_to_all(tiles, axes, split_axis=0, concat_axis=0, tiled=True)  40.8 us
    unnamed x38, local copies, waits for them, and re-layouts  15.9 us
    all_to_all x1, starting transfers between devices, exchange(): return lax.all_to_all(tiles, axes, split_axis=0, concat_axis=0, tiled=True)  13.2 us
    pallas_call x1, Pallas kernels, encode(): call(functools.partial(encode_body, chunk), (jax.ShapeDtypeStruct((peers,...  7.84 us
    pallas_call x1, Pallas kernels, gradient(): call(gradient_body, (jax.ShapeDtypeStruct((half, features), BF), jax.Shap...  2.96 us
    all_gather x1, blocking collectives, shards(): gathered = lax.all_gather(gathered, 'c', axis=0, tiled=True)  2.51 us
    pallas_call x1, Pallas kernels, prepare(): call(functools.partial(prepare_body, blocks), (jax.ShapeDtypeStruct((half...  2.14 us
  transfers between devices with their start and end apart: 5, of which 2 were waited for; matrix products, arithmetic and copies ran while one was open for 0% of the time, Pallas kernels for 2%

profile of v1, /device:TPU:8, one launch (start us, length us, event | category | flops | bytes accessed | tf_op | source)
XLA Modules:
  0.0 91.5 jit_solution(15911531249087053990)
XLA Ops:
  1.3 0.0 copy-start
  1.3 1.7 %copy-done = bf16[1536,768]{1,0:T(8,128)(2,1)S(1)} copy-done((bf16[1536,768]{1,0:T(8,128)(2,1)S(1)}, bf16[1536,768]{1,0:T(8,128)(2,1)}, u32[]{:S(2)}) %copy-start) | copy-done | bytes 2359320
  2.9 0.0 copy-start.2
  2.9 1.7 %copy-done.2 = bf16[1536,768]{1,0:T(8,128)(2,1)S(1)} copy-done((bf16[1536,768]{1,0:T(8,128)(2,1)S(1)}, bf16[1536,768]{1,0:T(8,128)(2,1)}, u32[]{:S(2)}) %copy-start.2) | copy-done | bytes 2359320
  4.6 0.0 copy-start.4
  4.6 0.9 %copy-done.4 = bf16[1,1,128,768]{3,2,1,0:T(8,128)(2,1)S(1)} copy-done((bf16[1,1,128,768]{3,2,1,0:T(8,128)(2,1)S(1)}, bf16[1,1,128,768]{3,2,1,0:T(8,128)(2,1)}, u32[]{:S(2)}) %copy-start.4) | copy-done | bytes 196632
  5.5 0.0 copy-start.6
  5.5 0.9 %copy-done.6 = bf16[1,1,128,768]{3,2,1,0:T(8,128)(2,1)S(1)} copy-done((bf16[1,1,128,768]{3,2,1,0:T(8,128)(2,1)S(1)}, bf16[1,1,128,768]{3,2,1,0:T(8,128)(2,1)}, u32[]{:S(2)}) %copy-start.6) | copy-done | bytes 196632
  6.5 0.0 copy-start.18
  6.5 0.7 copy-done.18
  7.1 0.0 copy-start.5
  7.1 0.0 copy-start.7
  7.1 0.0 copy-start.1
  7.1 7.8 %shard_map.77 = (bf16[64,16,128]{2,1,0:T(8,128)(2,1)}, bf16[256,768]{1,0:T(8,128)(2,1)S(1)}, f32[8,256]{1,0:T(8,128)S(1)}) custom-call(s32[1,1]{1,0:T(1,128)S(6)} %copy.8.pos, s32[1,2]{1,0:T(1,128)S(1)} %bitcast.18, bf16[128,768]{1,0:T(8,128)(2,1)S(1)} %bitcast.8, bf16[128,768]{1,0:T(8,128)(2,1)S(1)} %bitcast.12, bf16[1536,768]{1,0:T(8,128)(2,1)S(1)} %copy-done, ...), custom_call_target="tpu_custom_call" | custom-call | tf_op jit(solution)/shard_map/pallas_call | solution.py:93
  15.0 13.2 %all-to-all-start = ((bf16[64,16,128]{2,1,0:T(8,128)(2,1)}), bf16[64,16,128]{2,1,0:T(8,128)(2,1)}, u32[]{:S(2)}, u32[]{:S(2)}) async-start(bf16[64,16,128]{2,1,0:T(8,128)(2,1)} %get-tuple-element.12), calls=%async_computation | async-start | bytes 524288 | tf_op jit(solution)/shard_map/all_to_all | solution.py:275
  28.2 0.1 collective-permute-start.2
  28.3 0.0 copy-done.5
  28.3 0.5 collective-permute-start
  28.8 0.0 copy-done.7
  28.8 0.1 collective-permute-start.1
  28.9 0.4 collective-permute-start.3
  29.3 1.3 %collective-permute-done.3.inv_s = f32[8,256]{1,0:T(8,128)S(1)} collective-permute-done((f32[8,256]{1,0:T(8,128)S(1)}, f32[8,256]{1,0:T(8,128)S(1)}, u32[]{:S(2)}, u32[]{:S(2)}) %collective-permute-start.3) | collective-permute-done | bytes 8224 | tf_op jit(solution)/shard_map/ppermute | solution.py:290
  30.6 0.0 collective-permute-done.qs
  30.6 0.0 collective-permute-done.1.ps
  30.6 0.0 collective-permute-done.2.normed_s
  30.6 0.0 copy-done.1
  30.6 0.0 copy-start.3
  30.6 1.7 %copy-done.3 = bf16[1536,768]{1,0:T(8,128)(2,1)S(1)} copy-done((bf16[1536,768]{1,0:T(8,128)(2,1)S(1)}, bf16[1536,768]{1,0:T(8,128)(2,1)}, u32[]{:S(2)}) %copy-start.3) | copy-done | bytes 2359320
  32.3 2.1 %shard_map.78 = (bf16[768,512]{1,0:T(8,128)(2,1)S(1)}, bf16[768,512]{1,0:T(8,128)(2,1)S(1)}, bf16[768,768]{1,0:T(8,128)(2,1)S(1)}) custom-call(bf16[128,768]{1,0:T(8,128)(2,1)S(1)} %bitcast.10, bf16[128,768]{1,0:T(8,128)(2,1)S(1)} %bitcast.14, bf16[128,768]{1,0:T(8,128)(2,1)S(1)} %collective-permute-done.qs, bf16[128,768]{1,0:T(8,128)(2,1)S(1)} %collective-permute-done.1.ps, ...), custom_call_target="tpu_custom_call" | custom-call | tf_op jit(solution)/shard_map/pallas_call | solution.py:141
  34.4 0.0 copy-start.8
  34.5 1.0 %copy-done.8 = bf16[768,768]{1,0:T(8,128)(2,1)} copy-done((bf16[768,768]{1,0:T(8,128)(2,1)}, bf16[768,768]{1,0:T(8,128)(2,1)S(1)}, u32[]{:S(2)}) %copy-start.8) | copy-done | bytes 1179672
  35.5 0.0 copy-start.10
  35.5 0.7 copy-done.10
  36.2 0.7 copy-done.12
  36.9 0.9 copy-done.14
  37.7 0.9 copy-done.16
  38.6 1.3 %all-to-all-done = bf16[64,16,128]{2,1,0:T(8,128)(2,1)} async-done(((bf16[64,16,128]{2,1,0:T(8,128)(2,1)}), bf16[64,16,128]{2,1,0:T(8,128)(2,1)}, u32[]{:S(2)}, u32[]{:S(2)}) %all-to-all-start) | async-done | bytes 262176 | tf_op jit(solution)/shard_map/all_to_all | solution.py:275
  39.9 2.5 %all_gather.3 = bf16[128,16,128]{2,1,0:T(8,128)(2,1)S(1)} all-gather(bf16[64,16,128]{2,1,0:T(8,128)(2,1)} %all-to-all-done), channel_id=1, replica_groups=mesh['y'=4,'xl'=2,'z'=8,'c'=2,'xh'=2] {'c'}, dimensions={0}, use_global_device_ids=true | all-gather | bytes 786432 | tf_op jit(solution)/shard_map/all_gather | solution.py:292
  42.4 0.0 copy-done.15
  42.5 1.3 %copy-done.9 = bf16[768,768]{1,0:T(8,128)(2,1)S(1)} copy-done((bf16[768,768]{1,0:T(8,128)(2,1)S(1)}, bf16[768,768]{1,0:T(8,128)(2,1)}, u32[]{:S(2)}) %copy-start.9) | copy-done | bytes 1179672
  43.7 0.9 %copy-done.11 = bf16[128,768]{1,0:T(8,128)(2,1)S(1)} copy-done((bf16[128,768]{1,0:T(8,128)(2,1)S(1)}, bf16[128,768]{1,0:T(8,128)(2,1)}, u32[]{:S(2)}) %copy-start.11) | copy-done | bytes 196632
  44.7 0.9 %copy-done.13 = bf16[128,768]{1,0:T(8,128)(2,1)S(1)} copy-done((bf16[128,768]{1,0:T(8,128)(2,1)S(1)}, bf16[128,768]{1,0:T(8,128)(2,1)}, u32[]{:S(2)}) %copy-start.13) | copy-done | bytes 196632
  45.6 1.1 %copy-done.17 = bf16[768,512]{1,0:T(8,128)(2,1)S(1)} copy-done((bf16[768,512]{1,0:T(8,128)(2,1)S(1)}, bf16[768,512]{1,0:T(8,128)(2,1)}, u32[]{:S(2)}) %copy-start.17) | copy-done | bytes 786456
  46.7 3.0 %shard_map.79 = (bf16[768,768]{1,0:T(8,128)(2,1)S(1)}, f32[8,128]{1,0:T(8,128)S(1)}) custom-call(bf16[2048,128]{1,0:T(8,128)(2,1)S(1)} %bitcast.7, bf16[768,512]{1,0:T(8,128)(2,1)S(1)} %copy-done.15, bf16[768,512]{1,0:T(8,128)(2,1)S(1)} %copy-done.17, bf16[768,768]{1,0:T(8,128)(2,1)S(1)} %copy-done.9, bf16[128,768]{1,0:T(8,128)(2,1)S(1)} %bitcast.11, ...), custom_call_target="tpu_custom_call" | custom-call | tf_op jit(solution)/shard_map/pallas_call | solution.py:209
  49.7 21.3 %all_to_all.15.arrived = bf16[8,96,768]{2,1,0:T(8,128)(2,1)S(1)} all-to-all(bf16[8,96,768]{2,1,0:T(8,128)(2,1)S(1)} %bitcast.16), channel_id=1, replica_groups=mesh['y'=4,'xl'=2,'z'=8,'c'=2,'xh'=2] {'y','xl'}, dimensions={0} | all-to-all | bytes 2359296 | tf_op jit(solution)/shard_map/all_to_all | solution.py:275
  70.9 0.3 shard_map.80
  71.3 19.6 %all_to_all.16.arrived = bf16[16,8,768]{2,1,0:T(8,128)(2,1)S(1)} all-to-all(bf16[16,8,768]{2,1,0:T(8,128)(2,1)S(1)} %bitcast.17), channel_id=1, replica_groups=mesh['y'=4,'xl'=2,'z'=8,'c'=2,'xh'=2] {'z','xh'}, dimensions={0} | all-to-all | bytes 393216 | tf_op jit(solution)/shard_map/all_to_all | solution.py:275
  90.8 0.6 shard_map.81
  (8 shorter events, 0.0 us)
Async XLA Ops:
  1.3 1.7 %copy-start = (bf16[1536,768]{1,0:T(8,128)(2,1)S(1)}, bf16[1536,768]{1,0:T(8,128)(2,1)}, u32[]{:S(2)}) copy-start(bf16[1536,768]{1,0:T(8,128)(2,1)} %wu.1) | copy-start | bytes 7077892
  2.9 1.7 %copy-start.2 = (bf16[1536,768]{1,0:T(8,128)(2,1)S(1)}, bf16[1536,768]{1,0:T(8,128)(2,1)}, u32[]{:S(2)}) copy-start(bf16[1536,768]{1,0:T(8,128)(2,1)} %wd.1) | copy-start | bytes 7077892
  4.6 0.9 %copy-start.4 = (bf16[1,1,128,768]{3,2,1,0:T(8,128)(2,1)S(1)}, bf16[1,1,128,768]{3,2,1,0:T(8,128)(2,1)}, u32[]{:S(2)}) copy-start(bf16[1,1,128,768]{3,2,1,0:T(8,128)(2,1)} %param.6) | copy-start | bytes 589828
  5.5 0.9 %copy-start.6 = (bf16[1,1,128,768]{3,2,1,0:T(8,128)(2,1)S(1)}, bf16[1,1,128,768]{3,2,1,0:T(8,128)(2,1)}, u32[]{:S(2)}) copy-start(bf16[1,1,128,768]{3,2,1,0:T(8,128)(2,1)} %param.7) | copy-start | bytes 589828
  6.5 0.7 copy-start.18
  7.1 21.2 %copy-start.5 = (bf16[1,1,128,768]{3,2,1,0:T(8,128)(2,1)S(1)}, bf16[1,1,128,768]{3,2,1,0:T(8,128)(2,1)}, u32[]{:S(2)}) copy-start(bf16[1,1,128,768]{3,2,1,0:T(8,128)(2,1)} %param.6) | copy-start | bytes 589828
  7.1 21.7 %copy-start.7 = (bf16[1,1,128,768]{3,2,1,0:T(8,128)(2,1)S(1)}, bf16[1,1,128,768]{3,2,1,0:T(8,128)(2,1)}, u32[]{:S(2)}) copy-start(bf16[1,1,128,768]{3,2,1,0:T(8,128)(2,1)} %param.7) | copy-start | bytes 589828
  7.1 23.5 %copy-start.1 = (bf16[1536,768]{1,0:T(8,128)(2,1)S(1)}, bf16[1536,768]{1,0:T(8,128)(2,1)}, u32[]{:S(2)}) copy-start(bf16[1536,768]{1,0:T(8,128)(2,1)} %wu.1) | copy-start | bytes 7077892
  15.0 25.0 %all-to-all-start = ((bf16[64,16,128]{2,1,0:T(8,128)(2,1)}), bf16[64,16,128]{2,1,0:T(8,128)(2,1)}, u32[]{:S(2)}, u32[]{:S(2)}) async-start(bf16[64,16,128]{2,1,0:T(8,128)(2,1)} %get-tuple-element.12), calls=%async_computation | async-start | bytes 524288 | tf_op jit(solution)/shard_map/all_to_all | solution.py:275
  28.2 2.4 %collective-permute-start.2 = (bf16[256,768]{1,0:T(8,128)(2,1)S(1)}, bf16[256,768]{1,0:T(8,128)(2,1)S(1)}, u32[]{:S(2)}, u32[]{:S(2)}) collective-permute-start(bf16[256,768]{1,0:T(8,128)(2,1)S(1)} %get-tuple-element.13.normed), channel_id=1, source_target_pairs={{0,2},{2,0},{1,3},{3,1},{4,6},{6,4},{5,7},{7,5},{8,10},{10,8},{9,1... | collective-permute-start | bytes 1179656 | tf_op jit(solution)/shard_map/ppermute | solution.py:290
  28.3 2.3 %collective-permute-start = (bf16[128,768]{1,0:T(8,128)(2,1)S(1)}, bf16[128,768]{1,0:T(8,128)(2,1)S(1)}, u32[]{:S(2)}, u32[]{:S(2)}) collective-permute-start(bf16[128,768]{1,0:T(8,128)(2,1)S(1)} %bitcast.9), channel_id=1, source_target_pairs={{0,2},{2,0},{1,3},{3,1},{4,6},{6,4},{5,7},{7,5},{8,10},{10,8},{9,1... | collective-permute-start | bytes 589832 | tf_op jit(solution)/shard_map/ppermute | solution.py:287
  28.8 1.8 %collective-permute-start.1 = (bf16[128,768]{1,0:T(8,128)(2,1)S(1)}, bf16[128,768]{1,0:T(8,128)(2,1)S(1)}, u32[]{:S(2)}, u32[]{:S(2)}) collective-permute-start(bf16[128,768]{1,0:T(8,128)(2,1)S(1)} %bitcast.13), channel_id=1, source_target_pairs={{0,2},{2,0},{1,3},{3,1},{4,6},{6,4},{5,7},{7,5},{8,10},{10,8},{9,1... | collective-permute-start | bytes 589832 | tf_op jit(solution)/shard_map/ppermute | solution.py:287
  28.9 1.7 %collective-permute-start.3 = (f32[8,256]{1,0:T(8,128)S(1)}, f32[8,256]{1,0:T(8,128)S(1)}, u32[]{:S(2)}, u32[]{:S(2)}) collective-permute-start(f32[8,256]{1,0:T(8,128)S(1)} %get-tuple-element.14.inv), channel_id=1, source_target_pairs={{0,2},{2,0},{1,3},{3,1},{4,6},{6,4},{5,7},{7,5},{8,10},{10,8},{9,1... | collective-permute-start | bytes 24584 | tf_op jit(solution)/shard_map/ppermute | solution.py:290
  30.6 1.7 %copy-start.3 = (bf16[1536,768]{1,0:T(8,128)(2,1)S(1)}, bf16[1536,768]{1,0:T(8,128)(2,1)}, u32[]{:S(2)}) copy-start(bf16[1536,768]{1,0:T(8,128)(2,1)} %wd.1) | copy-start | bytes 7077892
  34.4 1.0 %copy-start.8 = (bf16[768,768]{1,0:T(8,128)(2,1)}, bf16[768,768]{1,0:T(8,128)(2,1)S(1)}, u32[]{:S(2)}) copy-start(bf16[768,768]{1,0:T(8,128)(2,1)S(1)} %get-tuple-element.17.wd) | copy-start | bytes 3538948
  35.5 0.7 copy-start.10
  36.2 0.7 copy-start.12
  36.9 0.9 copy-start.14
  37.7 0.9 copy-start.16
  39.9 2.5 %copy-start.15 = (bf16[768,512]{1,0:T(8,128)(2,1)S(1)}, bf16[768,512]{1,0:T(8,128)(2,1)}, u32[]{:S(2)}) copy-start(bf16[768,512]{1,0:T(8,128)(2,1)} %copy-done.14) | copy-start | bytes 2359300
  42.5 1.3 %copy-start.9 = (bf16[768,768]{1,0:T(8,128)(2,1)S(1)}, bf16[768,768]{1,0:T(8,128)(2,1)}, u32[]{:S(2)}) copy-start(bf16[768,768]{1,0:T(8,128)(2,1)} %copy-done.8) | copy-start | bytes 3538948
  43.7 0.9 %copy-start.11 = (bf16[128,768]{1,0:T(8,128)(2,1)S(1)}, bf16[128,768]{1,0:T(8,128)(2,1)}, u32[]{:S(2)}) copy-start(bf16[128,768]{1,0:T(8,128)(2,1)} %copy-done.10) | copy-start | bytes 589828
  44.6 0.9 %copy-start.13 = (bf16[128,768]{1,0:T(8,128)(2,1)S(1)}, bf16[128,768]{1,0:T(8,128)(2,1)}, u32[]{:S(2)}) copy-start(bf16[128,768]{1,0:T(8,128)(2,1)} %copy-done.12) | copy-start | bytes 589828
  45.6 1.1 %copy-start.17 = (bf16[768,512]{1,0:T(8,128)(2,1)S(1)}, bf16[768,512]{1,0:T(8,128)(2,1)}, u32[]{:S(2)}) copy-start(bf16[768,512]{1,0:T(8,128)(2,1)} %copy-done.16) | copy-start | bytes 2359300

commit v2 on v1

--- a/solution.py
+++ b/solution.py
@@ -21,8 +21,7 @@
 MIB = 1 << 20
 
 WHOLE = pl.BlockSpec(memory_space=pltpu.VMEM)
-SCALARS = pl.BlockSpec(memory_space=pltpu.SMEM)
-ANYWHERE = pl.BlockSpec(memory_space=pl.ANY)
+IN_HBM = pl.BlockSpec(memory_space=pltpu.HBM)
 
 SPAN = 16
 
@@ -31,40 +30,58 @@
     return lax.dot_general(left, right, (((1,), (1,)), ((), ())), preferred_element_type=F32)
 
 
-def call(body, outs, ins, scratch=(), vmem=24):
+def start_all(copies):
+    for copy in copies:
+        copy.start()
+    return copies
+
+
+def wait_all(copies):
+    for copy in copies:
+        copy.wait()
+
+
+def in_hbm(*arrays):
+    return [pltpu.with_memory_space_constraint(a, pltpu.HBM) for a in arrays]
+
+
+def call(body, outs, ins, scratch=(), vmem=24, place=None):
     return pl.pallas_call(
         body,
         out_shape=outs,
         in_specs=ins,
-        out_specs=jax.tree.map(lambda _: WHOLE, outs),
+        out_specs=jax.tree.map(lambda _: WHOLE, outs) if place is None else place,
         scratch_shapes=scratch,
         compiler_params=pltpu.CompilerParams(vmem_limit_bytes=vmem * MIB),
     )
 
 
-def encode_body(chunk, pos, hard, q, p, wu_hbm, wd_hbm, message, normed_out, inv_out, wu, wd, sem_u, sem_d):
+def encode_body(chunk, pos, hard_hbm, q, p, wu_hbm, wd_hbm, message, normed_out, inv_out, both, wu, wd, hard, sem, sem_u, sem_d):
     hidden_units, features = wu.shape
+    length = q.shape[0]
     steps = hidden_units // chunk
-
-    def copies(n):
+    own = start_all(
+        [
+            pltpu.make_async_copy(q, both.at[pl.ds(0, length)], sem.at[0]),
+            pltpu.make_async_copy(p, both.at[pl.ds(length, length)], sem.at[1]),
+        ]
+    )
+    ups, downs = [], []
+    for n in range(steps):
         at = pl.ds(n * chunk, chunk)
-        return (
-            pltpu.make_async_copy(wu_hbm.at[at], wu.at[at], sem_u.at[n]),
-            pltpu.make_async_copy(wd_hbm.at[at], wd.at[at], sem_d.at[n]),
-        )
-
-    for n in range(steps):
-        for copy in copies(n):
-            copy.start()
-    tokens = jnp.concatenate([q[...], p[...]], 0)
+        ups.append(pltpu.make_async_copy(wu_hbm.at[at], wu.at[at], sem_u.at[n]))
+        downs.append(pltpu.make_async_copy(wd_hbm.at[at], wd.at[at], sem_d.at[n]))
+        start_all([ups[-1], downs[-1]])
+    indices = start_all([pltpu.make_async_copy(hard_hbm, hard, sem.at[2])])
+    wait_all(own)
+    tokens = both[...]
     summed = tokens.astype(F32)
     for n in range(steps):
         at = pl.ds(n * chunk, chunk)
-        up, down = copies(n)
-        up.wait()
+        ups[n].wait()
         pre_act = rows_by_rows(tokens, wu[at, :])
         hidden = (0.5 * pre_act * (1.0 + lax.erf(pre_act * SQRT_HALF))).astype(BF)
-        down.wait()
+        downs[n].wait()
         summed = summed + jnp.dot(hidden, wd[at, :], preferred_element_type=F32)
     row_mean = jnp.mean(summed, -1, keepdims=True)
     centred = summed - row_mean
@@ -72,7 +89,7 @@
     normed = centred * inv_scale
     normed_out[...] = normed.astype(BF)
     inv_out[...] = jnp.transpose(jnp.broadcast_to(inv_scale, (inv_scale.shape[0], 128)))[:8]
-    length = q.shape[0]
+    wait_all(indices)
     rows = []
     for s in range(2):
         embed = jnp.mean(normed[s * length : (s + 1) * length], 0, keepdims=True)
@@ -97,66 +114,127 @@
             jax.ShapeDtypeStruct((2 * length, features), BF),
             jax.ShapeDtypeStruct((8, 2 * length), F32),
         ),
-        [SCALARS, SCALARS, WHOLE, WHOLE, ANYWHERE, ANYWHERE],
-        [
+        [pl.BlockSpec(memory_space=pltpu.SMEM)] + [IN_HBM] * 5,
+        [
+            pltpu.VMEM((2 * length, features), BF),
             pltpu.VMEM((hidden_units, features), BF),
             pltpu.VMEM((hidden_units, features), BF),
+            pltpu.SMEM(hard.shape, jnp.int32),
+            pltpu.SemaphoreType.DMA((3,)),
             pltpu.SemaphoreType.DMA((steps,)),
             pltpu.SemaphoreType.DMA((steps,)),
         ],
-    )(pos, hard, q, p, w_up, w_down)
-
-
-def prepare_body(blocks, q, p, qs, ps, normed, normed_s, inv, inv_s, wu, wd, slope_out, along_out, wd_out, wu_mine):
+    )(pos, *in_hbm(hard, q, p, w_up, w_down))
+
+
+def prepare_body(blocks, q, p, qs, ps, normed, normed_s, inv, inv_s, wu_hbm, wd_hbm, slope_hbm, along_hbm, wd_out, tokens_out, normed_out, wu, wd, wu_mine, wd_mine, tokens, normed_all, slope_all, along_all, sem_w, sem_t, sem_o, sem_n):
     core = lax.axis_index("c")
-    features = wu.shape[1]
     width = wu.shape[0] // blocks
     half = width // 2
+    length = q.shape[0]
+    ups, downs = [], []
+    for n in range(2):
+        at = pl.ds(n * (wu.shape[0] // 2), wu.shape[0] // 2)
+        ups.append(pltpu.make_async_copy(wu_hbm.at[at], wu.at[at], sem_w.at[n]))
+        downs.append(pltpu.make_async_copy(wd_hbm.at[at], wd.at[at], sem_w.at[2 + n]))
+    start_all(ups)
+    moves = start_all(
+        [
+            pltpu.make_async_copy(part, tokens.at[pl.ds(k * length, length)], sem_t.at[k])
+            for k, part in enumerate((q, p))
+        ]
+    )
+    start_all(downs)
+    tokens[2 * length : 3 * length] = qs[...]
+    tokens[3 * length :] = ps[...]
+    normed_all[: 2 * length] = normed[...]
+    normed_all[2 * length :] = normed_s[...]
     mine = lax.broadcasted_iota(jnp.int32, (half, width), 0)
     source = lax.broadcasted_iota(jnp.int32, (half, width), 1)
     run = half // 8
     skipped = sum((mine >= run * k).astype(jnp.int32) for k in range(1, 8))
     pick = (source == mine + run * (skipped + core)).astype(F32).astype(BF)
-    for b in range(blocks):
-        old, new = pl.ds(b * width, width), pl.ds(b * half, half)
-        wu_mine[new, :] = jnp.dot(pick, wu[old, :], preferred_element_type=F32).astype(BF)
-        wd_out[new, :] = jnp.dot(pick, wd[old, :], preferred_element_type=F32).astype(BF)
-    tokens = jnp.concatenate([q[...], p[...], qs[...], ps[...]], 0)
-    normed_all = jnp.concatenate([normed[...], normed_s[...]], 0)
+    def pick_rows(copies, weights, to):
+        for b in range(blocks):
+            if b % (blocks // 2) == 0:
+                copies[b // (blocks // 2)].wait()
+            rows = jnp.dot(pick, weights[pl.ds(b * width, width), :], preferred_element_type=F32)
+            to[pl.ds(b * half, half), :] = rows.astype(BF)
+
+    pick_rows(ups, wu, wu_mine)
+    wait_all(moves)
+    leaving = start_all(
+        [
+            pltpu.make_async_copy(tokens, tokens_out, sem_o.at[0]),
+            pltpu.make_async_copy(normed_all, normed_out, sem_o.at[1]),
+        ]
+    )
+    pick_rows(downs, wd, wd_mine)
+    leaving += start_all([pltpu.make_async_copy(wd_mine, wd_out, sem_o.at[2])])
     inv_all = jnp.concatenate([inv[0:1, :], inv_s[0:1, :]], 1)
     chunk = 256
     for n in range(wu_mine.shape[0] // chunk):
         at = pl.ds(n * chunk, chunk)
-        pre_act = rows_by_rows(wu_mine[at, :], tokens)
+        pre_act = rows_by_rows(wu_mine[at, :], tokens[...])
         slope = 0.5 * (1.0 + lax.erf(pre_act * SQRT_HALF))
         slope = slope + pre_act * jnp.exp(-0.5 * pre_act * pre_act) * DENSITY
         scaled = slope * inv_all
-        slope_out[at, :] = scaled.astype(BF)
-        along_out[at, :] = (scaled * rows_by_rows(wd_out[at, :], normed_all)).astype(BF)
+        slope_all[at, :] = scaled.astype(BF)
+        along_all[at, :] = (scaled * rows_by_rows(wd_mine[at, :], normed_all[...])).astype(BF)
+        leaving += start_all(
+            [
+                pltpu.make_async_copy(slope_all.at[at], slope_hbm.at[at], sem_n.at[0, n]),
+                pltpu.make_async_copy(along_all.at[at], along_hbm.at[at], sem_n.at[1, n]),
+            ]
+        )
+    wait_all(leaving)
 
 
 def prepare(blocks, q, p, qs, ps, normed, normed_s, inv, inv_s, w_up, w_down):
     hidden_units, features = w_up.shape
     half, count = hidden_units // 2, 4 * q.shape[0]
+    shapes = ((half, count), (half, count), (half, features), (count, features), (count, features))
     return call(
         functools.partial(prepare_body, blocks),
-        (
-            jax.ShapeDtypeStruct((half, count), BF),
-            jax.ShapeDtypeStruct((half, count), BF),
-            jax.ShapeDtypeStruct((half, features), BF),
-        ),
-        [WHOLE] * 10,
-        [pltpu.VMEM((half, features), BF)],
+        tuple(pltpu.HBM(shape, BF) for shape in shapes),
+        [IN_HBM] * 2 + [WHOLE] * 6 + [IN_HBM] * 2,
+        [
+            pltpu.VMEM((hidden_units, features), BF),
+            pltpu.VMEM((hidden_units, features), BF),
+            pltpu.VMEM((half, features), BF),
+            pltpu.VMEM((half, features), BF),
+            pltpu.VMEM((count, features), BF),
+            pltpu.VMEM((count, features), BF),
+            pltpu.VMEM((half, count), BF),
+            pltpu.VMEM((half, count), BF),
+            pltpu.SemaphoreType.DMA((4,)),
+            pltpu.SemaphoreType.DMA((2,)),
+            pltpu.SemaphoreType.DMA((3,)),
+            pltpu.SemaphoreType.DMA((2, half // 256)),
+        ],
         vmem=28,
-    )(q, p, qs, ps, normed, normed_s, inv, inv_s, w_up, w_down)
-
-
-def gradient_body(gathered, slope, along, wd, q, p, qs, ps, normed, normed_s, terms, loss, wide, d_query, d_passage):
+        place=(IN_HBM,) * 5,
+    )(*in_hbm(q, p), qs, ps, normed, normed_s, inv, inv_s, *in_hbm(w_up, w_down))
+
+
+def gradient_body(length, gathered, slope_hbm, along_hbm, wd_hbm, tokens_hbm, normed_hbm, terms, loss, wide, d_query, d_passage, slope, along, wd, tokens, normed_all, sem):
+    arriving = {
+        name: pltpu.make_async_copy(source, to, sem.at[k])
+        for k, (name, source, to) in enumerate(
+            (
+                ("normed", normed_hbm, normed_all),
+                ("wd", wd_hbm, wd),
+                ("slope", slope_hbm, slope),
+                ("along", along_hbm, along),
+                ("tokens", tokens_hbm, tokens),
+            )
+        )
+    }
+    start_all(arriving.values())
     core = lax.axis_index("c")
     place = (lax.axis_index("y") * 2 + lax.axis_index("xl")) * 8 + lax.axis_index("z")
     pool, features = d_query.shape
     cores_apart = pool // 2
-    length = q.shape[0]
     wide[...] = gathered[...].astype(F32)
     parts = features // 128
     from_all = lambda k: wide[pl.ds(k, pool, stride=SPAN), :]
@@ -188,9 +266,12 @@
     high = both.astype(BF)
     low = (both - high.astype(F32)).astype(BF)
     vectors = jnp.concatenate([high, low], 0)
-    normed_all = jnp.concatenate([normed[...], normed_s[...]], 0)
-    shares = rows_by_rows(vectors, normed_all)
+    arriving["normed"].wait()
+    shares = rows_by_rows(vectors, normed_all[...])
+    arriving["wd"].wait()
     offsets = rows_by_rows(wd[...], vectors)
+    arriving["slope"].wait()
+    arriving["along"].wait()
     pieces = []
     for s in range(4):
         at = slice(s * length, (s + 1) * length)
@@ -199,23 +280,25 @@
         piece = offset * slope[:, at].astype(F32) - share * along[:, at].astype(F32)
         pieces.append(piece.astype(BF))
     grad_pre = jnp.concatenate(pieces, 1)
-    tokens = jnp.concatenate([q[...], p[...], qs[...], ps[...]], 0)
-    terms[...] = jnp.dot(grad_pre, tokens, preferred_element_type=F32).astype(BF)
-
-
-def gradient(gathered, slope, along, wd, q, p, qs, ps, normed, normed_s):
+    arriving["tokens"].wait()
+    terms[...] = jnp.dot(grad_pre, tokens[...], preferred_element_type=F32).astype(BF)
+
+
+def gradient(length, gathered, slope, along, wd, tokens, normed):
     half, features = wd.shape
     pool = gathered.shape[0] // SPAN
     return call(
-        gradient_body,
+        functools.partial(gradient_body, length),
         (jax.ShapeDtypeStruct((half, features), BF), jax.ShapeDtypeStruct((8, 128), F32)),
-        [WHOLE] * 10,
+        [WHOLE] + [IN_HBM] * 5,
         [
             pltpu.VMEM(gathered.shape, F32),
             pltpu.VMEM((pool, features), F32),
             pltpu.VMEM((pool, features), F32),
+            *(pltpu.VMEM(a.shape, BF) for a in (slope, along, wd, tokens, normed)),
+            pltpu.SemaphoreType.DMA((5,)),
         ],
-    )(gathered, slope, along, wd, q, p, qs, ps, normed, normed_s)
+    )(gathered, *in_hbm(slope, along, wd, tokens, normed))
 
 
 def add_near_body(own_rows, arrived, loss, out):
@@ -288,10 +371,10 @@
     message, normed, inv = encode(pos_index, hard_index.reshape(1, -1), q, p, w_up, w_down, peers)
     gathered = exchange(message, ("y", "xl", "z"))
     normed_s, inv_s = (lax.ppermute(a, "c", SWAP) for a in (normed, inv))
-    slope, along, wd = prepare(near_count, q, p, qs, ps, normed, normed_s, inv, inv_s, w_up, w_down)
+    slope, along, wd, tokens, normed_all = prepare(near_count, q, p, qs, ps, normed, normed_s, inv, inv_s, w_up, w_down)
     gathered = lax.all_gather(gathered, "c", axis=0, tiled=True)
     terms, loss = gradient(
-        gathered.reshape(-1, 128), slope, along, wd, q, p, qs, ps, normed, normed_s
+        q.shape[0], gathered.reshape(-1, 128), slope, along, wd, tokens, normed_all
     )
     arrived = exchange(terms.reshape(near_count, -1, features), near)
     partial = add_near(arrived, loss, own_rows)

time: 92 us -> 79.6 us (0.87)
  local copies, waits for them, and re-layouts: 15.9 us -> 0.01 us
  Pallas kernels: 13.9 us -> 18.2 us
  blocking collectives: 43.3 us -> 40.4 us
  waiting for transfers between devices: 2.57 us -> 5.19 us
    unnamed x38 -> x4, local copies, waits for them, and re-layouts: 15.9 us -> 0.01 us
    pallas_call x2, Pallas kernels: 5.11 us -> 9.97 us  [the longest x1 5.48 us: prepare(): call(functools.partial(prepare_body, blocks), tuple((pltpu.HBM(shape, BF)...]
    all_to_all x1, waiting for transfers between devices: 1.29 us -> 3.92 us  [exchange(): return lax.all_to_all(tiles, axes, split_axis=0, concat_axis=0, tiled=True)]
    all_to_all x2, blocking collectives: 40.8 us -> 38.2 us  [exchange(): return lax.all_to_all(tiles, axes, split_axis=0, concat_axis=0, tiled=True)]
  transfers between devices with their start and end apart: 5 -> 5, of which waited for: 2 -> 2; matrix products, arithmetic and copies ran while one was open for 0% -> 0% of each run, Pallas kernels for 2% -> 7%
where the time goes in v2:
time: 79.6 us; the launch traced here: 79.3 us
  blocking collectives  40.4 us (51%)
  Pallas kernels  18.2 us (23%)
  starting transfers between devices  14.1 us (18%)
  waiting for transfers between devices  5.19 us (7%)
  between operations  1.36 us (2%)
    all_to_all x2, blocking collectives, exchange(): return lax.all_to_all(tiles, axes, split_axis=0, concat_axis=0, tiled=True)  38.2 us
    all_to_all x1, starting transfers between devices, exchange(): return lax.all_to_all(tiles, axes, split_axis=0, concat_axis=0, tiled=True)  13 us
    pallas_call x1, Pallas kernels, encode(): call(functools.partial(encode_body, chunk), (jax.ShapeDtypeStruct((peers,...  7.31 us
    pallas_call x1, Pallas kernels, prepare(): call(functools.partial(prepare_body, blocks), tuple((pltpu.HBM(shape, BF)...  5.48 us
    pallas_call x1, Pallas kernels, gradient(): call(functools.partial(gradient_body, length), (jax.ShapeDtypeStruct((hal...  4.49 us
    all_to_all x1, waiting for transfers between devices, exchange(): return lax.all_to_all(tiles, axes, split_axis=0, concat_axis=0, tiled=True)  3.92 us
    all_gather x1, blocking collectives, shards(): gathered = lax.all_gather(gathered, 'c', axis=0, tiled=True)  2.17 us
  transfers between devices with their start and end apart: 5, of which 2 were waited for; matrix products, arithmetic and copies ran while one was open for 0% of the time, Pallas kernels for 7%

profile of v2, /device:TPU:8, one launch (start us, length us, event | category | flops | bytes accessed | tf_op | source)
XLA Modules:
  0.0 79.3 jit_solution(1698810903217422883)
XLA Ops:
  1.3 0.0 copy-start
  1.3 0.0 copy-start.1
  1.3 7.3 %shard_map.77 = (bf16[64,16,128]{2,1,0:T(8,128)(2,1)}, bf16[256,768]{1,0:T(8,128)(2,1)S(1)}, f32[8,256]{1,0:T(8,128)S(1)}) custom-call(s32[1,1]{1,0:T(1,128)S(6)} %copy.8.pos, s32[1,2]{1,0:T(1,128)} %bitcast.16, bf16[128,768]{1,0:T(8,128)(2,1)} %bitcast.10, bf16[128,768]{1,0:T(8,128)(2,1)} %bitcast.13, bf16[1536,768]{1,0:T(8,128)(2,1)} %wu_hbm.3, ...), custom_call_target="tpu_custom_call" | custom-call | tf_op jit(solution)/shard_map/pallas_call | solution.py:110
  8.6 13.0 %all-to-all-start = ((bf16[64,16,128]{2,1,0:T(8,128)(2,1)}), bf16[64,16,128]{2,1,0:T(8,128)(2,1)S(1)}, u32[]{:S(2)}, u32[]{:S(2)}) async-start(bf16[64,16,128]{2,1,0:T(8,128)(2,1)} %get-tuple-element.14), calls=%async_computation | async-start | bytes 524288 | tf_op jit(solution)/shard_map/all_to_all | solution.py:358
  21.7 0.1 collective-permute-start.2
  21.8 0.0 copy-done
  21.8 0.5 collective-permute-start
  22.3 0.0 copy-done.1
  22.3 0.1 collective-permute-start.1
  22.4 0.4 collective-permute-start.3
  22.8 1.3 %collective-permute-done.3.inv_s = f32[8,256]{1,0:T(8,128)S(1)} collective-permute-done((f32[8,256]{1,0:T(8,128)S(1)}, f32[8,256]{1,0:T(8,128)S(1)}, u32[]{:S(2)}, u32[]{:S(2)}) %collective-permute-start.3) | collective-permute-done | bytes 8224 | tf_op jit(solution)/shard_map/ppermute | solution.py:373
  24.1 0.0 collective-permute-done.qs
  24.1 0.0 collective-permute-done.1.ps
  24.1 0.0 collective-permute-done.2.normed_s
  24.1 5.5 %shard_map.78 = (bf16[768,512]{1,0:T(8,128)(2,1)}, bf16[768,512]{1,0:T(8,128)(2,1)}, bf16[768,768]{1,0:T(8,128)(2,1)}, bf16[512,768]{1,0:T(8,128)(2,1)}, bf16[512,768]{1,0:T(8,128)(2,1)}) custom-call(bf16[128,768]{1,0:T(8,128)(2,1)} %bitcast.11, bf16[128,768]{1,0:T(8,128)(2,1)} %bitcast.14, bf16[128,768]{1,0:T(8,128)(2,1)S(1)} %collective-permute-done.qs, ...), custom_call_target="tpu_custom_call" | custom-call | tf_op jit(solution)/shard_map/pallas_call | solution.py:197
  29.6 3.9 %all-to-all-done = bf16[64,16,128]{2,1,0:T(8,128)(2,1)S(1)} async-done(((bf16[64,16,128]{2,1,0:T(8,128)(2,1)}), bf16[64,16,128]{2,1,0:T(8,128)(2,1)S(1)}, u32[]{:S(2)}, u32[]{:S(2)}) %all-to-all-start) | async-done | bytes 262176 | tf_op jit(solution)/shard_map/all_to_all | solution.py:358
  33.5 2.2 %all_gather.3 = bf16[128,16,128]{2,1,0:T(8,128)(2,1)S(1)} all-gather(bf16[64,16,128]{2,1,0:T(8,128)(2,1)S(1)} %all-to-all-done), channel_id=1, replica_groups=mesh['y'=4,'xl'=2,'z'=8,'c'=2,'xh'=2] {'c'}, dimensions={0}, use_global_device_ids=true | all-gather | bytes 786432 | tf_op jit(solution)/shard_map/all_gather | solution.py:375
  35.6 4.5 %shard_map.79 = (bf16[768,768]{1,0:T(8,128)(2,1)S(1)}, f32[8,128]{1,0:T(8,128)S(1)}) custom-call(bf16[2048,128]{1,0:T(8,128)(2,1)S(1)} %bitcast.7, bf16[768,512]{1,0:T(8,128)(2,1)} %get-tuple-element.17.slope_hbm, bf16[768,512]{1,0:T(8,128)(2,1)} %get-tuple-element.18.along_hbm, bf16[768,768]{1,0:T(8,128)(2,1)} %get-tuple-element.19.wd_hbm, ...), custom_call_target="tpu_custom_call" | custom-call | tf_op jit(solution)/shard_map/pallas_call | solution.py:290
  40.1 21.3 %all_to_all.15.arrived = bf16[8,96,768]{2,1,0:T(8,128)(2,1)S(1)} all-to-all(bf16[8,96,768]{2,1,0:T(8,128)(2,1)S(1)} %bitcast.8), channel_id=1, replica_groups=mesh['y'=4,'xl'=2,'z'=8,'c'=2,'xh'=2] {'y','xl'}, dimensions={0} | all-to-all | bytes 2359296 | tf_op jit(solution)/shard_map/all_to_all | solution.py:358
  61.4 0.3 shard_map.80
  61.7 17.0 %all_to_all.16.arrived = bf16[16,8,768]{2,1,0:T(8,128)(2,1)S(1)} all-to-all(bf16[16,8,768]{2,1,0:T(8,128)(2,1)S(1)} %bitcast.9), channel_id=1, replica_groups=mesh['y'=4,'xl'=2,'z'=8,'c'=2,'xh'=2] {'z','xh'}, dimensions={0} | all-to-all | bytes 393216 | tf_op jit(solution)/shard_map/all_to_all | solution.py:358
  78.7 0.6 shard_map.81
Async XLA Ops:
  1.3 20.5 %copy-start = (bf16[1,1,128,768]{3,2,1,0:T(8,128)(2,1)S(1)}, bf16[1,1,128,768]{3,2,1,0:T(8,128)(2,1)}, u32[]{:S(2)}) copy-start(bf16[1,1,128,768]{3,2,1,0:T(8,128)(2,1)} %param.6) | copy-start | bytes 589828
  1.3 21.0 %copy-start.1 = (bf16[1,1,128,768]{3,2,1,0:T(8,128)(2,1)S(1)}, bf16[1,1,128,768]{3,2,1,0:T(8,128)(2,1)}, u32[]{:S(2)}) copy-start(bf16[1,1,128,768]{3,2,1,0:T(8,128)(2,1)} %param.7) | copy-start | bytes 589828
  8.6 24.9 %all-to-all-start = ((bf16[64,16,128]{2,1,0:T(8,128)(2,1)}), bf16[64,16,128]{2,1,0:T(8,128)(2,1)S(1)}, u32[]{:S(2)}, u32[]{:S(2)}) async-start(bf16[64,16,128]{2,1,0:T(8,128)(2,1)} %get-tuple-element.14), calls=%async_computation | async-start | bytes 524288 | tf_op jit(solution)/shard_map/all_to_all | solution.py:358
  21.7 2.4 %collective-permute-start.2 = (bf16[256,768]{1,0:T(8,128)(2,1)S(1)}, bf16[256,768]{1,0:T(8,128)(2,1)S(1)}, u32[]{:S(2)}, u32[]{:S(2)}) collective-permute-start(bf16[256,768]{1,0:T(8,128)(2,1)S(1)} %get-tuple-element.15.normed), channel_id=1, source_target_pairs={{0,2},{2,0},{1,3},{3,1},{4,6},{6,4},{5,7},{7,5},{8,10},{10,8},{9,1... | collective-permute-start | bytes 1179656 | tf_op jit(solution)/shard_map/ppermute | solution.py:373
  21.8 2.3 %collective-permute-start = (bf16[128,768]{1,0:T(8,128)(2,1)S(1)}, bf16[128,768]{1,0:T(8,128)(2,1)S(1)}, u32[]{:S(2)}, u32[]{:S(2)}) collective-permute-start(bf16[128,768]{1,0:T(8,128)(2,1)S(1)} %bitcast.12), channel_id=1, source_target_pairs={{0,2},{2,0},{1,3},{3,1},{4,6},{6,4},{5,7},{7,5},{8,10},{10,8},{9,1... | collective-permute-start | bytes 589832 | tf_op jit(solution)/shard_map/ppermute | solution.py:370
  22.3 1.8 %collective-permute-start.1 = (bf16[128,768]{1,0:T(8,128)(2,1)S(1)}, bf16[128,768]{1,0:T(8,128)(2,1)S(1)}, u32[]{:S(2)}, u32[]{:S(2)}) collective-permute-start(bf16[128,768]{1,0:T(8,128)(2,1)S(1)} %bitcast.15), channel_id=1, source_target_pairs={{0,2},{2,0},{1,3},{3,1},{4,6},{6,4},{5,7},{7,5},{8,10},{10,8},{9,1... | collective-permute-start | bytes 589832 | tf_op jit(solution)/shard_map/ppermute | solution.py:370
  22.4 1.7 %collective-permute-start.3 = (f32[8,256]{1,0:T(8,128)S(1)}, f32[8,256]{1,0:T(8,128)S(1)}, u32[]{:S(2)}, u32[]{:S(2)}) collective-permute-start(f32[8,256]{1,0:T(8,128)S(1)} %get-tuple-element.16.inv), channel_id=1, source_target_pairs={{0,2},{2,0},{1,3},{3,1},{4,6},{6,4},{5,7},{7,5},{8,10},{10,8},{9,1... | collective-permute-start | bytes 24584 | tf_op jit(solution)/shard_map/ppermute | solution.py:373

commit v3 on v2

v3 whole, which is shorter than its diff:
```python
import functools
import math

import jax
import jax.numpy as jnp
from jax import lax
from jax.experimental import pallas as pl
from jax.experimental.pallas import tpu as pltpu
from jax.sharding import Mesh
from jax.sharding import PartitionSpec as P


DP = ("y", "xl", "z", "c")
SWAP = ((0, 1), (1, 0))

norm_eps = 1e-06
HARD_BOOST = 1.5
SQRT_HALF = 1.0 / math.sqrt(2.0)
DENSITY = 1.0 / math.sqrt(2.0 * math.pi)
BF = jnp.bfloat16
F32 = jnp.float32
MIB = 1 << 20

WHOLE = pl.BlockSpec(memory_space=pltpu.VMEM)
IN_HBM = pl.BlockSpec(memory_space=pltpu.HBM)

SPAN = 16
SPARE = 16


def rows_by_rows(left, right):
    return lax.dot_general(left, right, (((1,), (1,)), ((), ())), preferred_element_type=F32)


def start_all(copies):
    for copy in copies:
        copy.start()
    return copies


def wait_all(copies):
    for copy in copies:
        copy.wait()


def in_hbm(*arrays):
    return [pltpu.with_memory_space_constraint(a, pltpu.HBM) for a in arrays]


def call(body, outs, ins, scratch=(), vmem=24, place=None, flops=0):
    return pl.pallas_call(
        body,
        out_shape=outs,
        in_specs=ins,
        out_specs=jax.tree.map(lambda _: WHOLE, outs) if place is None else place,
        scratch_shapes=scratch,
        cost_estimate=pl.CostEstimate(flops=flops, transcendentals=0, bytes_accessed=0),
        compiler_params=pltpu.CompilerParams(vmem_limit_bytes=vmem * MIB),
    )


def split(value):
    first = value.astype(BF).astype(F32)
    second = (value - first).astype(BF).astype(F32)
    return first, second, value - first - second


def encode_body(chunk, pos, hard_hbm, q, p, wu_hbm, wd_hbm, message, shared, wu, wd, hard, sem, sem_u, sem_d):
    hidden_units, features = wu.shape
    length = q.shape[0]
    count = 2 * length
    steps = hidden_units // chunk
    own = start_all(
        [
            pltpu.make_async_copy(q, shared.at[pl.ds(0, length)], sem.at[0]),
            pltpu.make_async_copy(p, shared.at[pl.ds(length, length)], sem.at[1]),
        ]
    )
    ups, downs = [], []
    for n in range(steps):
        at = pl.ds(n * chunk, chunk)
        ups.append(pltpu.make_async_copy(wu_hbm.at[at], wu.at[at], sem_u.at[n]))
        downs.append(pltpu.make_async_copy(wd_hbm.at[at], wd.at[at], sem_d.at[n]))
        start_all([ups[-1], downs[-1]])
    indices = start_all([pltpu.make_async_copy(hard_hbm, hard, sem.at[2])])
    wait_all(own)
    tokens = shared[:count]
    summed = tokens.astype(F32)
    for n in range(steps):
        at = pl.ds(n * chunk, chunk)
        ups[n].wait()
        pre_act = rows_by_rows(tokens, wu[at, :])
        hidden = (0.5 * pre_act * (1.0 + lax.erf(pre_act * SQRT_HALF))).astype(BF)
        downs[n].wait()
        summed = summed + jnp.dot(hidden, wd[at, :], preferred_element_type=F32)
    row_mean = jnp.mean(summed, -1, keepdims=True)
    centred = summed - row_mean
    inv_scale = lax.rsqrt(jnp.mean(centred * centred, -1, keepdims=True) + norm_eps)
    normed = centred * inv_scale
    shared[count : 2 * count] = normed.astype(BF)
    inv_row = jnp.transpose(jnp.broadcast_to(inv_scale, (count, 128)))[:1]
    pieces = jnp.concatenate([*split(inv_row), jnp.zeros((SPARE - 3, count), F32)], 0)
    shared[2 * count :, :count] = pieces.astype(BF)
    shared[2 * count :, count:] = jnp.zeros((SPARE, features - count), BF)
    wait_all(indices)
    rows = []
    for s in range(2):
        embed = jnp.mean(normed[s * length : (s + 1) * length], 0, keepdims=True)
        rows += [embed[:, k * 128 : (k + 1) * 128] for k in range(features // 128)]
    lane = lax.broadcasted_iota(jnp.int32, (1, 128), 1)
    index_row = jnp.where(lane == 0, pos[0, 0], jnp.where(lane == 1, hard[0, 0], hard[0, 1]))
    rows.append(index_row.astype(F32))
    rows.append(jnp.zeros((SPAN - len(rows), 128), F32))
    block = jnp.concatenate(rows, 0).astype(BF)
    message[...] = jnp.broadcast_to(block[None], message.shape)


def encode(pos, hard, q, p, w_up, w_down, peers):
    length, features = q.shape
    hidden_units = w_up.shape[0]
    chunk = hidden_units // 2
    steps = hidden_units // chunk
    return call(
        functools.partial(encode_body, chunk),
        (
            jax.ShapeDtypeStruct((peers, SPAN, 128), BF),
            jax.ShapeDtypeStruct((4 * length + SPARE, features), BF),
        ),
        [pl.BlockSpec(memory_space=pltpu.SMEM)] + [IN_HBM] * 5,
        [
            pltpu.VMEM((hidden_units, features), BF),
            pltpu.VMEM((hidden_units, features), BF),
            pltpu.SMEM(hard.shape, jnp.int32),
            pltpu.SemaphoreType.DMA((3,)),
            pltpu.SemaphoreType.DMA((steps,)),
            pltpu.SemaphoreType.DMA((steps,)),
        ],
    )(pos, *in_hbm(hard, q, p, w_up, w_down))


def prepare_body(blocks, shared, shared_s, wu_hbm, wd_hbm, slope_hbm, tokens_hbm, wd_out, along, normed_all, wu, wd, wu_mine, wd_mine, tokens, slope_all, sem_u, sem_d, sem_o):
    core = lax.axis_index("c")
    width = wu.shape[0] // blocks
    half = width // 2
    count = tokens.shape[0] // 2
    ups, downs = [], []
    parts = 2
    for n in range(parts):
        at = pl.ds(n * (wu.shape[0] // parts), wu.shape[0] // parts)
        ups.append(pltpu.make_async_copy(wu_hbm.at[at], wu.at[at], sem_u.at[n]))
        downs.append(pltpu.make_async_copy(wd_hbm.at[at], wd.at[at], sem_d.at[n]))
    start_all(ups)
    tokens[:count] = shared[:count]
    tokens[count:] = shared_s[:count]
    normed_all[:count] = shared[count : 2 * count]
    normed_all[count:] = shared_s[count : 2 * count]
    mine = lax.broadcasted_iota(jnp.int32, (half, width), 0)
    source = lax.broadcasted_iota(jnp.int32, (half, width), 1)
    run = half // 8
    skipped = sum((mine >= run * k).astype(jnp.int32) for k in range(1, 8))
    pick = (source == mine + run * (skipped + core)).astype(F32).astype(BF)
    def pick_rows(copies, weights, to, then=()):
        for b in range(blocks):
            if b % (blocks // parts) == 0:
                copies[b // (blocks // parts)].wait()
                start_all(then[b // (blocks // parts) :][:1])
            rows = jnp.dot(pick, weights[pl.ds(b * width, width), :], preferred_element_type=F32)
            to[pl.ds(b * half, half), :] = rows.astype(BF)

    leaving = start_all([pltpu.make_async_copy(tokens, tokens_hbm, sem_o.at[0])])
    pick_rows(ups, wu, wu_mine, downs)
    pre_act = rows_by_rows(wu_mine[...], tokens[...])
    pick_rows(downs, wd, wd_mine)
    leaving += start_all([pltpu.make_async_copy(wd_mine, wd_out, sem_o.at[2])])
    inv_all = jnp.concatenate(
        [jnp.sum(a[2 * count :, :count].astype(F32), 0, keepdims=True) for a in (shared, shared_s)], 1
    )
    slope = 0.5 * (1.0 + lax.erf(pre_act * SQRT_HALF))
    slope = slope + pre_act * jnp.exp(-0.5 * pre_act * pre_act) * DENSITY
    scaled = slope * inv_all
    slope_all[...] = scaled.astype(BF)
    leaving += start_all([pltpu.make_async_copy(slope_all, slope_hbm, sem_o.at[1])])
    along[...] = (scaled * rows_by_rows(wd_mine[...], normed_all[...])).astype(BF)
    wait_all(leaving)


def prepare(blocks, shared, shared_s, w_up, w_down):
    hidden_units, features = w_up.shape
    half, count = hidden_units // 2, (shared.shape[0] - SPARE)
    shapes = ((half, count), (count, features), (half, features))
    return call(
        functools.partial(prepare_body, blocks),
        (
            *(pltpu.HBM(shape, BF) for shape in shapes),
            jax.ShapeDtypeStruct((half, count), BF),
            jax.ShapeDtypeStruct((count, features), BF),
        ),
        [WHOLE] * 2 + [IN_HBM] * 2,
        [
            pltpu.VMEM((hidden_units, features), BF),
            pltpu.VMEM((hidden_units, features), BF),
            pltpu.VMEM((half, features), BF),
            pltpu.VMEM((half, features), BF),
            pltpu.VMEM((count, features), BF),
            pltpu.VMEM((half, count), BF),
            pltpu.SemaphoreType.DMA((2,)),
            pltpu.SemaphoreType.DMA((2,)),
            pltpu.SemaphoreType.DMA((3,)),
        ],
        vmem=28,
        place=(IN_HBM,) * 3 + (WHOLE,) * 2,
        flops=8 * half * count * features,
    )(shared, shared_s, *in_hbm(w_up, w_down))


def gradient_body(length, gathered, along, normed_all, wd_hbm, slope_hbm, tokens_hbm, terms, loss, wide, d_query, d_passage, wd, slope, tokens, sem):
    arriving = start_all(
        [
            pltpu.make_async_copy(source, to, sem.at[k])
            for k, (source, to) in enumerate(
                ((wd_hbm, wd), (slope_hbm, slope), (tokens_hbm, tokens))
            )
        ]
    )
    core = lax.axis_index("c")
    place = (lax.axis_index("y") * 2 + lax.axis_index("xl")) * 8 + lax.axis_index("z")
    pool, features = d_query.shape
    cores_apart = pool // 2
    wide[...] = gathered[...].astype(F32)
    parts = features // 128
    from_all = lambda k: wide[pl.ds(k, pool, stride=SPAN), :]
    queries = jnp.concatenate([from_all(k) for k in range(parts)], 1).astype(BF)
    passages = jnp.concatenate([from_all(parts + k) for k in range(parts)], 1).astype(BF)
    indices = from_all(2 * parts)
    lane = lax.broadcasted_iota(jnp.int32, (1, pool), 1)
    late = (lane >= cores_apart).astype(jnp.int32)
    column = (2 * (lane - cores_apart * late) + late).astype(F32)
    target = indices[:, 0:1] == column
    named = (indices[:, 1:2] == column) | (indices[:, 2:3] == column)
    logits = rows_by_rows(queries, passages) + jnp.where(named, HARD_BOOST, 0.0)
    row_max = jnp.max(logits, -1, keepdims=True)
    log_total = row_max + jnp.log(jnp.sum(jnp.exp(logits - row_max), -1, keepdims=True))
    picked = jnp.sum(jnp.where(target, logits, 0.0), -1, keepdims=True)
    loss[...] = jnp.broadcast_to(jnp.sum(log_total - picked, 0, keepdims=True), loss.shape)
    weights = (jnp.exp(logits - log_total) - jnp.where(target, 1.0, 0.0)).astype(BF)
    d_query[...] = jnp.dot(weights, passages, preferred_element_type=F32)
    d_passage[...] = lax.dot_general(
        weights, queries, (((0,), (0,)), ((), ())), preferred_element_type=F32
    )
    own = core * cores_apart + place
    sibling = (1 - core) * cores_apart + place
    grad = jnp.concatenate(
        [d[pl.ds(at, 1), :] for at in (own, sibling) for d in (d_query, d_passage)], 0
    ) * (1.0 / length)
    level = grad - jnp.mean(grad, -1, keepdims=True)
    both = jnp.concatenate([grad, level], 0)
    high = both.astype(BF)
    low = (both - high.astype(F32)).astype(BF)
    vectors = jnp.concatenate([high, low], 0)
    shares = rows_by_rows(vectors, normed_all[...])
    arriving[0].wait()
    offsets = rows_by_rows(wd[...], vectors)
    arriving[1].wait()
    pieces = []
    for s in range(4):
        at = slice(s * length, (s + 1) * length)
        share = (shares[s : s + 1, at] + shares[8 + s : 9 + s, at]) * (1.0 / features)
        offset = offsets[:, 4 + s : 5 + s] + offsets[:, 12 + s : 13 + s]
        piece = offset * slope[:, at].astype(F32) - share * along[:, at].astype(F32)
        pieces.append(piece.astype(BF))
    grad_pre = jnp.concatenate(pieces, 1)
    arriving[2].wait()
    terms[...] = jnp.dot(grad_pre, tokens[...], preferred_element_type=F32).astype(BF)


def gradient(length, gathered, along, normed, wd, slope, tokens):
    half, features = wd.shape
    pool = gathered.shape[0] // SPAN
    return call(
        functools.partial(gradient_body, length),
        (jax.ShapeDtypeStruct((half, features), BF), jax.ShapeDtypeStruct((8, 128), F32)),
        [WHOLE] * 3 + [IN_HBM] * 3,
        [
            pltpu.VMEM(gathered.shape, F32),
            pltpu.VMEM((pool, features), F32),
            pltpu.VMEM((pool, features), F32),
            *(pltpu.VMEM(a.shape, BF) for a in (wd, slope, tokens)),
            pltpu.SemaphoreType.DMA((3,)),
        ],
    )(gathered, along, normed, *in_hbm(wd, slope, tokens))


def add_near_body(own_rows, arrived, loss, out):
    senders, rows, features = arrived.shape
    total = arrived[0].astype(F32)
    for s in range(1, senders):
        total = total + arrived[s].astype(F32)
    groups = rows // own_rows
    spread = lax.broadcasted_iota(jnp.int32, (groups * 8, rows), 0)
    source = lax.broadcasted_iota(jnp.int32, (groups * 8, rows), 1)
    group = spread >> 3
    inner = spread & 7
    pick = ((inner < own_rows) & (source == own_rows * group + inner)).astype(F32).astype(BF)
    placed = jnp.dot(pick, total.astype(BF), preferred_element_type=F32)
    first, second, third = split(loss[0:1, 0:1])
    lane = lax.broadcasted_iota(jnp.int32, (1, features), 1)
    pieces = jnp.where(lane == 0, first, jnp.where(lane == 1, second, jnp.where(lane == 2, third, 0.0)))
    is_loss = (lax.broadcasted_iota(jnp.int32, (groups * 8, 1), 0) & 7) == own_rows
    out[...] = jnp.where(is_loss, pieces, placed).astype(BF)


def add_near(arrived, loss, own_rows):
    groups = arrived.shape[1] // own_rows
    return call(
        functools.partial(add_near_body, own_rows),
        jax.ShapeDtypeStruct((groups * 8, arrived.shape[2]), BF),
        [WHOLE] * 2,
    )(arrived, loss)


def add_far_body(count, arrived, rows, mean_loss):
    total = arrived[0].astype(F32)
    for s in range(1, arrived.shape[0]):
        total = total + arrived[s].astype(F32)
    own = rows.shape[0]
    rows[...] = total[:own]
    loss = arrived[0, own : own + 1, 0:128].astype(F32) + arrived[1, own : own + 1, 0:128].astype(F32)
    lane = lax.broadcasted_iota(jnp.int32, (1, 128), 1)
    mean_loss[...] = jnp.sum(jnp.where(lane < 3, loss, 0.0), -1, keepdims=True) * (1.0 / count)


def add_far(arrived, own_rows, count):
    return call(
        functools.partial(add_far_body, count),
        (
            jax.ShapeDtypeStruct((own_rows, arrived.shape[2]), F32),
            jax.ShapeDtypeStruct((1, 1), F32),
        ),
        [WHOLE],
    )(arrived)


def exchange(tiles, axes):
    return lax.all_to_all(tiles, axes, split_axis=0, concat_axis=0, tiled=True)


def step(q_hidden, p_hidden, w_up, w_down, pos_index, hard_index):
    features = w_up.shape[1]
    q = q_hidden.reshape(-1, features)
    p = p_hidden.reshape(-1, features)
    near, far = ("y", "xl"), ("z", "xh")
    near_count = lax.axis_size(near)
    far_count = lax.axis_size(far)
    own_rows = w_up.shape[0] // (2 * near_count * far_count)
    peers = lax.axis_size(("y", "xl", "z"))
    message, shared = encode(pos_index, hard_index.reshape(1, -1), q, p, w_up, w_down, peers)
    gathered = exchange(message, ("y", "xl", "z"))
    shared_s = lax.ppermute(shared, "c", SWAP)
    slope, tokens, wd, along, normed = prepare(near_count, shared, shared_s, w_up, w_down)
    gathered = lax.all_gather(gathered, "c", axis=0, tiled=True)
    terms, loss = gradient(
        q.shape[0], gathered.reshape(-1, 128), along, normed, wd, slope, tokens
    )
    arrived = exchange(terms.reshape(near_count, -1, features), near)
    partial = add_near(arrived, loss, own_rows)
    arrived = exchange(partial.reshape(far_count, 8, features), far)
    count = lax.axis_size(DP) * lax.axis_size("xh")
    rows, mean_loss = add_far(arrived, own_rows, count)
    return rows, mean_loss.reshape(())


def solution(mesh):
    finer = Mesh(mesh.devices.reshape(4, 2, 8, 2, mesh.shape["rep"]), ("y", "xl", "z", "c", "xh"))
    return jax.shard_map(
        step,
        mesh=finer,
        in_specs=(
            P("xh", DP, None, None),
            P("xh", DP, None, None),
            P(),
            P(),
            P("xh", DP),
            P("xh", DP, None),
        ),
        out_specs=(P((*DP, "xh"), None), P()),
        check_vma=False,
    )
```

time: 79.6 us -> 80.9 us (1.016)
  blocking collectives: 40.4 us -> 64.7 us
  starting transfers between devices: 14.1 us -> 0.09 us
  waiting for transfers between devices: 5.19 us -> 0.01 us
  Pallas kernels: 18.2 us -> 14.5 us
    all_to_all x2 -> x3, blocking collectives: 38.2 us -> 62.6 us  [exchange(): return lax.all_to_all(tiles, axes, split_axis=0, concat_axis=0, tiled=True)]
    all_to_all x1 -> x0, starting transfers between devices: 13 us -> none  [exchange(): return lax.all_to_all(tiles, axes, split_axis=0, concat_axis=0, tiled=True)]
    all_to_all x1 -> x0, waiting for transfers between devices: 3.92 us -> none  [exchange(): return lax.all_to_all(tiles, axes, split_axis=0, concat_axis=0, tiled=True)]
    pallas_call x1, Pallas kernels: 7.31 us -> 4.13 us  [encode(): call(functools.partial(encode_body, chunk), (jax.ShapeDtypeStruct((peers,...]
    ppermute x4 -> x1, waiting for transfers between devices: 1.28 us -> 0.01 us  [step(): shared_s = lax.ppermute(shared, 'c', SWAP)]
    ppermute x4 -> x1, starting transfers between devices: 1.09 us -> 0.09 us  [step(): shared_s = lax.ppermute(shared, 'c', SWAP)]
    pallas_call x1, Pallas kernels: 4.49 us -> 3.68 us  [gradient(): call(functools.partial(gradient_body, length), (jax.ShapeDtypeStruct((hal...]
  transfers between devices with their start and end apart: 5 -> 1, of which waited for: 2 -> 0; matrix products, arithmetic and copies ran while one was open for 0% -> 0% of each run, Pallas kernels for 7% -> 0%
where the time goes in v3:
time: 80.9 us; the launch traced here: 80.6 us
  blocking collectives  64.7 us (80%)
  Pallas kernels  14.5 us (18%)
  between operations  1.32 us (2%)
    all_to_all x3, blocking collectives, exchange(): return lax.all_to_all(tiles, axes, split_axis=0, concat_axis=0, tiled=True)  62.6 us
    pallas_call x1, Pallas kernels, prepare(): call(functools.partial(prepare_body, blocks), (*(pltpu.HBM(shape, BF) for...  5.69 us
    pallas_call x1, Pallas kernels, encode(): call(functools.partial(encode_body, chunk), (jax.ShapeDtypeStruct((peers,...  4.13 us
    pallas_call x1, Pallas kernels, gradient(): call(functools.partial(gradient_body, length), (jax.ShapeDtypeStruct((hal...  3.68 us
    all_gather x1, blocking collectives, step(): gathered = lax.all_gather(gathered, 'c', axis=0, tiled=True)  2.17 us
  transfers between devices with their start and end apart: 1, of which 0 were waited for; matrix products, arithmetic and copies ran while one was open for 0% of the time, Pallas kernels for 0%

profile of v3, /device:TPU:8, one launch (start us, length us, event | category | flops | bytes accessed | tf_op | source)
XLA Modules:
  0.0 80.6 jit_solution(15547379700678465628)
XLA Ops:
  1.3 4.1 %shard_map.77 = (bf16[64,16,128]{2,1,0:T(8,128)(2,1)S(1)}, bf16[528,768]{1,0:T(8,128)(2,1)S(1)}) custom-call(s32[1,1]{1,0:T(1,128)S(6)} %copy.8.pos, s32[1,2]{1,0:T(1,128)} %bitcast.12, bf16[128,768]{1,0:T(8,128)(2,1)} %bitcast.10, bf16[128,768]{1,0:T(8,128)(2,1)} %bitcast.11, bf16[1536,768]{1,0:T(8,128)(2,1)} %wu_hbm.3, bf16[1536,768]{1,0:T(8,128)(2,1)} %wd_hbm.3), custom_call_target="tpu_custom_call" | custom-call | tf_op jit(solution)/shard_map/pallas_call | solution.py:123
  5.4 0.1 collective-permute-start
  5.5 25.3 %all_to_all.15 = bf16[64,16,128]{2,1,0:T(8,128)(2,1)S(1)} all-to-all(bf16[64,16,128]{2,1,0:T(8,128)(2,1)S(1)} %get-tuple-element.13), channel_id=1, replica_groups=mesh['y'=4,'xl'=2,'z'=8,'c'=2,'xh'=2] {'y','xl','z'}, dimensions={0} | all-to-all | bytes 524288 | tf_op jit(solution)/shard_map/all_to_all | solution.py:344
  30.8 2.2 %all_gather.3 = bf16[128,16,128]{2,1,0:T(8,128)(2,1)S(1)} all-gather(bf16[64,16,128]{2,1,0:T(8,128)(2,1)S(1)} %all_to_all.15), channel_id=1, replica_groups=mesh['y'=4,'xl'=2,'z'=8,'c'=2,'xh'=2] {'c'}, dimensions={0}, use_global_device_ids=true | all-gather | bytes 786432 | tf_op jit(solution)/shard_map/all_gather | solution.py:360
  33.0 0.0 collective-permute-done.shared_s
  33.0 5.7 %shard_map.78 = (bf16[768,512]{1,0:T(8,128)(2,1)}, bf16[512,768]{1,0:T(8,128)(2,1)}, bf16[768,768]{1,0:T(8,128)(2,1)}, bf16[768,512]{1,0:T(8,128)(2,1)S(1)}, bf16[512,768]{1,0:T(8,128)(2,1)S(1)}) custom-call(bf16[528,768]{1,0:T(8,128)(2,1)S(1)} %get-tuple-element.14.shared, bf16[528,768]{1,0:T(8,128)(2,1)S(1)} %collective-permute-done.shared_s, ...), custom_call_target="tpu_custom_call" | custom-call | flops 2415919104 | tf_op jit(solution)/shard_map/pallas_call | solution.py:191
  38.7 3.7 %shard_map.79 = (bf16[768,768]{1,0:T(8,128)(2,1)S(1)}, f32[8,128]{1,0:T(8,128)S(1)}) custom-call(bf16[2048,128]{1,0:T(8,128)(2,1)S(1)} %bitcast.7, bf16[768,512]{1,0:T(8,128)(2,1)S(1)} %get-tuple-element.15.along, bf16[512,768]{1,0:T(8,128)(2,1)S(1)} %get-tuple-element.16.normed_all, bf16[768,768]{1,0:T(8,128)(2,1)} %get-tuple-element.17.wd_hbm, ...), custom_call_target="tpu_custom_call" | custom-call | tf_op jit(solution)/shard_map/pallas_call | solution.py:279
  42.4 21.3 %all_to_all.16.arrived = bf16[8,96,768]{2,1,0:T(8,128)(2,1)S(1)} all-to-all(bf16[8,96,768]{2,1,0:T(8,128)(2,1)S(1)} %bitcast.8), channel_id=1, replica_groups=mesh['y'=4,'xl'=2,'z'=8,'c'=2,'xh'=2] {'y','xl'}, dimensions={0} | all-to-all | bytes 2359296 | tf_op jit(solution)/shard_map/all_to_all | solution.py:344
  63.6 0.3 shard_map.80
  64.0 16.0 %all_to_all.17.arrived = bf16[16,8,768]{2,1,0:T(8,128)(2,1)S(1)} all-to-all(bf16[16,8,768]{2,1,0:T(8,128)(2,1)S(1)} %bitcast.9), channel_id=1, replica_groups=mesh['y'=4,'xl'=2,'z'=8,'c'=2,'xh'=2] {'z','xh'}, dimensions={0} | all-to-all | bytes 393216 | tf_op jit(solution)/shard_map/all_to_all | solution.py:344
  80.0 0.6 shard_map.81
Async XLA Ops:
  5.4 27.6 %collective-permute-start = (bf16[528,768]{1,0:T(8,128)(2,1)S(1)}, bf16[528,768]{1,0:T(8,128)(2,1)S(1)}, u32[]{:S(2)}, u32[]{:S(2)}) collective-permute-start(bf16[528,768]{1,0:T(8,128)(2,1)S(1)} %get-tuple-element.14.shared), channel_id=1, source_target_pairs={{0,2},{2,0},{1,3},{3,1},{4,6},{6,4},{5,7},{7,5},{8,10},{10,8},{9,1... | collective-permute-start | bytes 2433032 | tf_op jit(solution)/shard_map/ppermute | solution.py:358

commit v4 on v3

--- a/solution.py
+++ b/solution.py
@@ -65,7 +65,12 @@
     return first, second, value - first - second
 
 
-def encode_body(chunk, pos, hard_hbm, q, p, wu_hbm, wd_hbm, message, shared, wu, wd, hard, sem, sem_u, sem_d):
+def encode_body(chunk, *refs):
+    sends = len(refs) == 14
+    if sends:
+        pos, hard_hbm, q, p, wu_hbm, wd_hbm, message, shared, wu, wd, sem, sem_u, sem_d, hard = refs
+    else:
+        q, p, wu_hbm, wd_hbm, shared, wu, wd, sem, sem_u, sem_d = refs
     hidden_units, features = wu.shape
     length = q.shape[0]
     count = 2 * length
@@ -82,7 +87,7 @@
         ups.append(pltpu.make_async_copy(wu_hbm.at[at], wu.at[at], sem_u.at[n]))
         downs.append(pltpu.make_async_copy(wd_hbm.at[at], wd.at[at], sem_d.at[n]))
         start_all([ups[-1], downs[-1]])
-    indices = start_all([pltpu.make_async_copy(hard_hbm, hard, sem.at[2])])
+    indices = start_all([pltpu.make_async_copy(hard_hbm, hard, sem.at[2])] if sends else [])
     wait_all(own)
     tokens = shared[:count]
     summed = tokens.astype(F32)
@@ -102,6 +107,8 @@
     pieces = jnp.concatenate([*split(inv_row), jnp.zeros((SPARE - 3, count), F32)], 0)
     shared[2 * count :, :count] = pieces.astype(BF)
     shared[2 * count :, count:] = jnp.zeros((SPARE, features - count), BF)
+    if not sends:
+        return
     wait_all(indices)
     rows = []
     for s in range(2):
@@ -115,115 +122,171 @@
     message[...] = jnp.broadcast_to(block[None], message.shape)
 
 
-def encode(pos, hard, q, p, w_up, w_down, peers):
+def encode(q, p, w_up, w_down, indices=None, peers=0):
     length, features = q.shape
     hidden_units = w_up.shape[0]
     chunk = hidden_units // 2
     steps = hidden_units // chunk
-    return call(
-        functools.partial(encode_body, chunk),
-        (
-            jax.ShapeDtypeStruct((peers, SPAN, 128), BF),
-            jax.ShapeDtypeStruct((4 * length + SPARE, features), BF),
-        ),
+    shared = jax.ShapeDtypeStruct((4 * length + SPARE, features), BF)
+    scratch = [
+        pltpu.VMEM((hidden_units, features), BF),
+        pltpu.VMEM((hidden_units, features), BF),
+        pltpu.SemaphoreType.DMA((3,)),
+        pltpu.SemaphoreType.DMA((steps,)),
+        pltpu.SemaphoreType.DMA((steps,)),
+    ]
+    body = functools.partial(encode_body, chunk)
+    flops = 8 * length * features * hidden_units
+    if indices is None:
+        places = [WHOLE] * 2 + [IN_HBM] * 2
+        return call(body, shared, places, scratch, flops=flops)(q, p, *in_hbm(w_up, w_down))
+    pos, hard = indices
+    return call(
+        body,
+        (jax.ShapeDtypeStruct((peers, SPAN, 128), BF), shared),
         [pl.BlockSpec(memory_space=pltpu.SMEM)] + [IN_HBM] * 5,
+        [*scratch, pltpu.SMEM(hard.shape, jnp.int32)],
+        flops=flops,
+    )(pos, *in_hbm(hard, q, p, w_up, w_down))
+
+
+def slopes(count, pair, wu_mine, wd_mine, tokens, normed_all, slope_all, along, slope_hbm, sem, between=None):
+    pre_act = rows_by_rows(wu_mine[...], tokens[...])
+    if between is not None:
+        between()
+    inv_all = jnp.concatenate(
+        [jnp.sum(a[2 * count :, :count].astype(F32), 0, keepdims=True) for a in pair], 1
+    )
+    slope = 0.5 * (1.0 + lax.erf(pre_act * SQRT_HALF))
+    slope = slope + pre_act * jnp.exp(-0.5 * pre_act * pre_act) * DENSITY
+    scaled = slope * inv_all
+    slope_all[...] = scaled.astype(BF)
+    leaving = start_all([pltpu.make_async_copy(slope_all, slope_hbm, sem)])
+    along[...] = (scaled * rows_by_rows(wd_mine[...], normed_all[...])).astype(BF)
+    wait_all(leaving)
+
+
+def lay_out(count, pair, tokens, normed_all, tokens_hbm, normed_hbm, sem):
+    for k, shared in enumerate(pair):
+        tokens[k * count : (k + 1) * count] = shared[:count]
+        normed_all[k * count : (k + 1) * count] = shared[count : 2 * count]
+    return start_all(
         [
-            pltpu.VMEM((hidden_units, features), BF),
-            pltpu.VMEM((hidden_units, features), BF),
-            pltpu.SMEM(hard.shape, jnp.int32),
-            pltpu.SemaphoreType.DMA((3,)),
-            pltpu.SemaphoreType.DMA((steps,)),
-            pltpu.SemaphoreType.DMA((steps,)),
-        ],
-    )(pos, *in_hbm(hard, q, p, w_up, w_down))
-
-
-def prepare_body(blocks, shared, shared_s, wu_hbm, wd_hbm, slope_hbm, tokens_hbm, wd_out, along, normed_all, wu, wd, wu_mine, wd_mine, tokens, slope_all, sem_u, sem_d, sem_o):
+            pltpu.make_async_copy(tokens, tokens_hbm, sem.at[0]),
+            pltpu.make_async_copy(normed_all, normed_hbm, sem.at[1]),
+        ]
+    )
+
+
+def prepare_near_body(width, shared, shared_s, wu_hbm, wd_hbm, slope_hbm, tokens_hbm, normed_hbm, wd_out, along, wu_mine, wd_mine, wu, wd, tokens, normed_all, slope_all, sem_u, sem_d, sem_o):
     core = lax.axis_index("c")
-    width = wu.shape[0] // blocks
+    side = lax.axis_index("xl")
     half = width // 2
+    blocks = wu.shape[0] // width
     count = tokens.shape[0] // 2
-    ups, downs = [], []
-    parts = 2
-    for n in range(parts):
-        at = pl.ds(n * (wu.shape[0] // parts), wu.shape[0] // parts)
-        ups.append(pltpu.make_async_copy(wu_hbm.at[at], wu.at[at], sem_u.at[n]))
-        downs.append(pltpu.make_async_copy(wd_hbm.at[at], wd.at[at], sem_d.at[n]))
-    start_all(ups)
-    tokens[:count] = shared[:count]
-    tokens[count:] = shared_s[:count]
-    normed_all[:count] = shared[count : 2 * count]
-    normed_all[count:] = shared_s[count : 2 * count]
+
+    def copies(weights_hbm, weights, sem):
+        return [
+            pltpu.make_async_copy(
+                weights_hbm.at[pl.ds(pl.multiple_of((2 * b + side) * width, width), width)],
+                weights.at[pl.ds(b * width, width)],
+                sem.at[b],
+            )
+            for b in range(blocks)
+        ]
+
+    ups = start_all(copies(wu_hbm, wu, sem_u))
+    downs = start_all(copies(wd_hbm, wd, sem_d))
+    leaving = lay_out(count, (shared, shared_s), tokens, normed_all, tokens_hbm, normed_hbm, sem_o)
     mine = lax.broadcasted_iota(jnp.int32, (half, width), 0)
     source = lax.broadcasted_iota(jnp.int32, (half, width), 1)
     run = half // 8
     skipped = sum((mine >= run * k).astype(jnp.int32) for k in range(1, 8))
     pick = (source == mine + run * (skipped + core)).astype(F32).astype(BF)
-    def pick_rows(copies, weights, to, then=()):
+
+    def pick_rows(weights, to):
         for b in range(blocks):
-            if b % (blocks // parts) == 0:
-                copies[b // (blocks // parts)].wait()
-                start_all(then[b // (blocks // parts) :][:1])
             rows = jnp.dot(pick, weights[pl.ds(b * width, width), :], preferred_element_type=F32)
             to[pl.ds(b * half, half), :] = rows.astype(BF)
 
-    leaving = start_all([pltpu.make_async_copy(tokens, tokens_hbm, sem_o.at[0])])
-    pick_rows(ups, wu, wu_mine, downs)
-    pre_act = rows_by_rows(wu_mine[...], tokens[...])
-    pick_rows(downs, wd, wd_mine)
-    leaving += start_all([pltpu.make_async_copy(wd_mine, wd_out, sem_o.at[2])])
-    inv_all = jnp.concatenate(
-        [jnp.sum(a[2 * count :, :count].astype(F32), 0, keepdims=True) for a in (shared, shared_s)], 1
-    )
-    slope = 0.5 * (1.0 + lax.erf(pre_act * SQRT_HALF))
-    slope = slope + pre_act * jnp.exp(-0.5 * pre_act * pre_act) * DENSITY
-    scaled = slope * inv_all
-    slope_all[...] = scaled.astype(BF)
-    leaving += start_all([pltpu.make_async_copy(slope_all, slope_hbm, sem_o.at[1])])
-    along[...] = (scaled * rows_by_rows(wd_mine[...], normed_all[...])).astype(BF)
+    wait_all(ups)
+    pick_rows(wu, wu_mine)
+
+    def pick_downs():
+        wait_all(downs)
+        pick_rows(wd, wd_mine)
+        leaving.extend(start_all([pltpu.make_async_copy(wd_mine, wd_out, sem_o.at[2])]))
+
+    slopes(count, (shared, shared_s), wu_mine, wd_mine, tokens, normed_all, slope_all, along, slope_hbm, sem_o.at[3], pick_downs)
     wait_all(leaving)
 
 
-def prepare(blocks, shared, shared_s, w_up, w_down):
+def prepare_near(blocks, shared, shared_s, w_up, w_down):
     hidden_units, features = w_up.shape
-    half, count = hidden_units // 2, (shared.shape[0] - SPARE)
-    shapes = ((half, count), (count, features), (half, features))
-    return call(
-        functools.partial(prepare_body, blocks),
-        (
-            *(pltpu.HBM(shape, BF) for shape in shapes),
-            jax.ShapeDtypeStruct((half, count), BF),
-            jax.ShapeDtypeStruct((count, features), BF),
-        ),
+    quarter, count = hidden_units // 4, shared.shape[0] - SPARE
+    shapes = ((quarter, count), (count, features), (count, features), (quarter, features))
+    mine = jax.ShapeDtypeStruct((quarter, features), BF)
+    return call(
+        functools.partial(prepare_near_body, hidden_units // (2 * blocks)),
+        (*(pltpu.HBM(shape, BF) for shape in shapes), jax.ShapeDtypeStruct((quarter, count), BF), mine, mine),
         [WHOLE] * 2 + [IN_HBM] * 2,
         [
-            pltpu.VMEM((hidden_units, features), BF),
-            pltpu.VMEM((hidden_units, features), BF),
-            pltpu.VMEM((half, features), BF),
-            pltpu.VMEM((half, features), BF),
-            pltpu.VMEM((count, features), BF),
-            pltpu.VMEM((half, count), BF),
-            pltpu.SemaphoreType.DMA((2,)),
-            pltpu.SemaphoreType.DMA((2,)),
+            pltpu.VMEM((2 * quarter, features), BF),
+            pltpu.VMEM((2 * quarter, features), BF),
+            pltpu.VMEM((count, features), BF),
+            pltpu.VMEM((count, features), BF),
+            pltpu.VMEM((quarter, count), BF),
+            pltpu.SemaphoreType.DMA((blocks,)),
+            pltpu.SemaphoreType.DMA((blocks,)),
+            pltpu.SemaphoreType.DMA((4,)),
+        ],
+        place=(IN_HBM,) * 4 + (WHOLE,) * 3,
+        flops=8 * quarter * count * features,
+    )(shared, shared_s, *in_hbm(w_up, w_down))
+
+
+def prepare_far_body(shared, shared_s, wu_mine, wd_mine, slope_hbm, tokens_hbm, normed_hbm, along, tokens, normed_all, slope_all, sem_o):
+    count = tokens.shape[0] // 2
+    pair = (shared, shared_s)
+    leaving = lay_out(count, pair, tokens, normed_all, tokens_hbm, normed_hbm, sem_o)
+    slopes(count, pair, wu_mine, wd_mine, tokens, normed_all, slope_all, along, slope_hbm, sem_o.at[2])
+    wait_all(leaving)
+
+
+def prepare_far(shared, shared_s, wu_mine, wd_mine):
+    quarter, features = wu_mine.shape
+    count = shared.shape[0] - SPARE
+    shapes = ((quarter, count), (count, features), (count, features))
+    return call(
+        prepare_far_body,
+        (*(pltpu.HBM(shape, BF) for shape in shapes), jax.ShapeDtypeStruct((quarter, count), BF)),
+        [WHOLE] * 4,
+        [
+            pltpu.VMEM((count, features), BF),
+            pltpu.VMEM((count, features), BF),
+            pltpu.VMEM((quarter, count), BF),
             pltpu.SemaphoreType.DMA((3,)),
         ],
-        vmem=28,
-        place=(IN_HBM,) * 3 + (WHOLE,) * 2,
-        flops=8 * half * count * features,
-    )(shared, shared_s, *in_hbm(w_up, w_down))
-
-
-def gradient_body(length, gathered, along, normed_all, wd_hbm, slope_hbm, tokens_hbm, terms, loss, wide, d_query, d_passage, wd, slope, tokens, sem):
-    arriving = start_all(
-        [
-            pltpu.make_async_copy(source, to, sem.at[k])
-            for k, (source, to) in enumerate(
-                ((wd_hbm, wd), (slope_hbm, slope), (tokens_hbm, tokens))
-            )
-        ]
-    )
-    core = lax.axis_index("c")
-    place = (lax.axis_index("y") * 2 + lax.axis_index("xl")) * 8 + lax.axis_index("z")
+        place=(IN_HBM,) * 3 + (WHOLE,),
+        flops=8 * quarter * count * features,
+    )(shared, shared_s, wu_mine, wd_mine)
+
+
+def gradient_body(length, gathered, along, along_f, wd_hbm, slope_hbm, slope_f_hbm, tokens_hbm, tokens_f_hbm, normed_hbm, normed_f_hbm, terms, loss, wide, d_query, d_passage, wd, slope, tokens, normed_all, sem):
+    half = 4 * length
+    low, high = pl.ds(0, half), pl.ds(half, half)
+    order = (
+        (normed_hbm, normed_all.at[low]),
+        (normed_f_hbm, normed_all.at[high]),
+        (wd_hbm, wd),
+        (slope_hbm, slope.at[0]),
+        (slope_f_hbm, slope.at[1]),
+        (tokens_hbm, tokens.at[low]),
+        (tokens_f_hbm, tokens.at[high]),
+    )
+    arriving = start_all([pltpu.make_async_copy(*pair, sem.at[k]) for k, pair in enumerate(order)])
+    core, side = lax.axis_index("c"), lax.axis_index("xl")
+    row, layer = lax.axis_index("y"), lax.axis_index("z")
     pool, features = d_query.shape
     cores_apart = pool // 2
     wide[...] = gathered[...].astype(F32)
@@ -247,47 +310,56 @@
     d_passage[...] = lax.dot_general(
         weights, queries, (((0,), (0,)), ((), ())), preferred_element_type=F32
     )
-    own = core * cores_apart + place
-    sibling = (1 - core) * cores_apart + place
+    places = [
+        c * cores_apart + (row * 2 + x) * 8 + layer for x in (side, 1 - side) for c in (core, 1 - core)
+    ]
     grad = jnp.concatenate(
-        [d[pl.ds(at, 1), :] for at in (own, sibling) for d in (d_query, d_passage)], 0
+        [d[pl.ds(at, 1), :] for at in places for d in (d_query, d_passage)], 0
     ) * (1.0 / length)
+    count = 2 * len(places)
     level = grad - jnp.mean(grad, -1, keepdims=True)
     both = jnp.concatenate([grad, level], 0)
-    high = both.astype(BF)
-    low = (both - high.astype(F32)).astype(BF)
-    vectors = jnp.concatenate([high, low], 0)
+    first = both.astype(BF)
+    rest = (both - first.astype(F32)).astype(BF)
+    vectors = jnp.concatenate([first, rest], 0)
+    wait_all(arriving[:2])
     shares = rows_by_rows(vectors, normed_all[...])
-    arriving[0].wait()
+    arriving[2].wait()
     offsets = rows_by_rows(wd[...], vectors)
-    arriving[1].wait()
+    wait_all(arriving[3:5])
     pieces = []
-    for s in range(4):
+    for s in range(count):
         at = slice(s * length, (s + 1) * length)
-        share = (shares[s : s + 1, at] + shares[8 + s : 9 + s, at]) * (1.0 / features)
-        offset = offsets[:, 4 + s : 5 + s] + offsets[:, 12 + s : 13 + s]
-        piece = offset * slope[:, at].astype(F32) - share * along[:, at].astype(F32)
-        pieces.append(piece.astype(BF))
+        inside = slice((s % 4) * length, (s % 4 + 1) * length)
+        share = (shares[s : s + 1, at] + shares[2 * count + s : 2 * count + s + 1, at]) * (1.0 / features)
+        u, v = count + s, 3 * count + s
+        offset = offsets[:, u : u + 1] + offsets[:, v : v + 1]
+        toward = (along, along_f)[s // 4][:, inside].astype(F32)
+        pieces.append((offset * slope[s // 4, :, inside].astype(F32) - share * toward).astype(BF))
     grad_pre = jnp.concatenate(pieces, 1)
-    arriving[2].wait()
+    wait_all(arriving[5:])
     terms[...] = jnp.dot(grad_pre, tokens[...], preferred_element_type=F32).astype(BF)
 
 
-def gradient(length, gathered, along, normed, wd, slope, tokens):
-    half, features = wd.shape
+def gradient(length, gathered, along, along_f, wd, *saved):
+    quarter, features = wd.shape
     pool = gathered.shape[0] // SPAN
+    count = 8 * length
     return call(
         functools.partial(gradient_body, length),
-        (jax.ShapeDtypeStruct((half, features), BF), jax.ShapeDtypeStruct((8, 128), F32)),
-        [WHOLE] * 3 + [IN_HBM] * 3,
+        (jax.ShapeDtypeStruct((quarter, features), BF), jax.ShapeDtypeStruct((8, 128), F32)),
+        [WHOLE] * 3 + [IN_HBM] * 7,
         [
             pltpu.VMEM(gathered.shape, F32),
             pltpu.VMEM((pool, features), F32),
             pltpu.VMEM((pool, features), F32),
-            *(pltpu.VMEM(a.shape, BF) for a in (wd, slope, tokens)),
-            pltpu.SemaphoreType.DMA((3,)),
+            pltpu.VMEM((quarter, features), BF),
+            pltpu.VMEM((2, quarter, count // 2), BF),
+            pltpu.VMEM((count, features), BF),
+            pltpu.VMEM((count, features), BF),
+            pltpu.SemaphoreType.DMA((7,)),
         ],
-    )(gathered, along, normed, *in_hbm(wd, slope, tokens))
+    )(gathered, along, along_f, *in_hbm(wd, *saved))
 
 
 def add_near_body(own_rows, arrived, loss, out):
@@ -348,18 +420,26 @@
     features = w_up.shape[1]
     q = q_hidden.reshape(-1, features)
     p = p_hidden.reshape(-1, features)
-    near, far = ("y", "xl"), ("z", "xh")
+    near, far = "y", ("z", "xh")
     near_count = lax.axis_size(near)
     far_count = lax.axis_size(far)
-    own_rows = w_up.shape[0] // (2 * near_count * far_count)
+    own_rows = w_up.shape[0] // (4 * near_count * far_count)
     peers = lax.axis_size(("y", "xl", "z"))
-    message, shared = encode(pos_index, hard_index.reshape(1, -1), q, p, w_up, w_down, peers)
+    qx = lax.ppermute(q, "xl", SWAP)
+    px = lax.ppermute(p, "xl", SWAP)
+    indices = (pos_index, hard_index.reshape(1, -1))
+    message, shared = encode(q, p, w_up, w_down, indices, peers)
     gathered = exchange(message, ("y", "xl", "z"))
     shared_s = lax.ppermute(shared, "c", SWAP)
-    slope, tokens, wd, along, normed = prepare(near_count, shared, shared_s, w_up, w_down)
+    shared_x = encode(qx, px, w_up, w_down)
+    shared_xs = lax.ppermute(shared_x, "c", SWAP)
+    slope, tokens, normed, wd, along, wu_mine, wd_mine = prepare_near(
+        near_count, shared, shared_s, w_up, w_down
+    )
+    slope_f, tokens_f, normed_f, along_f = prepare_far(shared_x, shared_xs, wu_mine, wd_mine)
     gathered = lax.all_gather(gathered, "c", axis=0, tiled=True)
     terms, loss = gradient(
-        q.shape[0], gathered.reshape(-1, 128), along, normed, wd, slope, tokens
+        q.shape[0], gathered.reshape(-1, 128), along, along_f, wd, slope, slope_f, tokens, tokens_f, normed, normed_f
     )
     arrived = exchange(terms.reshape(near_count, -1, features), near)
     partial = add_near(arrived, loss, own_rows)

time: 80.9 us -> 86.2 us (1.066)
  blocking collectives: 64.7 us -> 57.9 us
  Pallas kernels: 14.5 us -> 20.2 us
  waiting for transfers between devices: 0.01 us -> 4.15 us
  starting transfers between devices: 0.09 us -> 2.3 us
    all_to_all x3, blocking collectives: 62.6 us -> 55.8 us  [exchange(): return lax.all_to_all(tiles, axes, split_axis=0, concat_axis=0, tiled=True)]
    pallas_call x3 -> x5, Pallas kernels: 13.5 us -> 19.3 us  [the longest x1 4.65 us: gradient(): call(functools.partial(gradient_body, length), (jax.ShapeDtypeStruct((qua...]
    ppermute x0 -> x3, waiting for transfers between devices: none -> 4.15 us  [the longest x1 3.08 us: step(): px = lax.ppermute(p, 'xl', SWAP)]
    ppermute x0 -> x3, starting transfers between devices: none -> 2.21 us  [the longest x1 1.58 us: step(): qx = lax.ppermute(q, 'xl', SWAP)]
  transfers between devices with their start and end apart: 1 -> 4, of which waited for: 0 -> 2; matrix products, arithmetic and copies ran while one was open for 0% -> 0% of each run, Pallas kernels for 0% -> 15%
where the time goes in v4:
time: 86.2 us; the launch traced here: 85.9 us
  blocking collectives  57.9 us (67%)
  Pallas kernels  20.2 us (23%)
  waiting for transfers between devices  4.15 us (5%)
  starting transfers between devices  2.3 us (3%)
  between operations  1.36 us (2%)
    all_to_all x3, blocking collectives, exchange(): return lax.all_to_all(tiles, axes, split_axis=0, concat_axis=0, tiled=True)  55.8 us
    pallas_call x1, Pallas kernels, gradient(): call(functools.partial(gradient_body, length), (jax.ShapeDtypeStruct((qua...  4.65 us
    pallas_call x1, Pallas kernels, prepare_near(): call(functools.partial(prepare_near_body, hidden_units // (2 * blocks)),...  4.51 us
    pallas_call x1, Pallas kernels, encode(): call(body, shared, places, scratch, flops=flops)  4.32 us
    pallas_call x1, Pallas kernels, encode(): call(body, (jax.ShapeDtypeStruct((peers, SPAN, 128), BF), shared), [pl.Bl...  4.13 us
    ppermute x1, waiting for transfers between devices, step(): px = lax.ppermute(p, 'xl', SWAP)  3.08 us
    all_gather x1, blocking collectives, step(): gathered = lax.all_gather(gathered, 'c', axis=0, tiled=True)  2.17 us
  transfers between devices with their start and end apart: 4, of which 2 were waited for; matrix products, arithmetic and copies ran while one was open for 0% of the time, Pallas kernels for 15%

profile of v4, /device:TPU:8, one launch (start us, length us, event | category | flops | bytes accessed | tf_op | source)
XLA Modules:
  0.0 85.9 jit_solution(3253243743333344183)
XLA Ops:
  0.6 1.6 %collective-permute-start.1 = (bf16[128,768]{1,0:T(8,128)(2,1)}, bf16[128,768]{1,0:T(8,128)(2,1)S(1)}, u32[]{:S(2)}, u32[]{:S(2)}) collective-permute-start(bf16[128,768]{1,0:T(8,128)(2,1)} %bitcast.10), channel_id=1, source_target_pairs={{0,32},{32,0},{1,33},{33,1},{2,34},{34,2},{3,35},{35,3},{4,36},{36... | collective-permute-start | bytes 589832 | tf_op jit(solution)/shard_map/ppermute | solution.py:428
  2.2 0.5 collective-permute-start.2
  3.4 4.1 %shard_map.77 = (bf16[64,16,128]{2,1,0:T(8,128)(2,1)S(1)}, bf16[528,768]{1,0:T(8,128)(2,1)S(1)}) custom-call(s32[1,1]{1,0:T(1,128)S(6)} %copy.8.refs_0_, s32[1,2]{1,0:T(1,128)} %bitcast.14, bf16[128,768]{1,0:T(8,128)(2,1)} %bitcast.11, bf16[128,768]{1,0:T(8,128)(2,1)} %bitcast.13, bf16[1536,768]{1,0:T(8,128)(2,1)} %refs_2_.1, bf16[1536,768]{1,0:T(8,128)(2,1)} %refs_3_.1), custom_call_target="tpu_custom_call" | custom-call | flops 1207959552 | tf_op jit(solution)/shard_map/pallas_call | solution.py:144
  7.5 0.1 collective-permute-start
  7.6 1.1 %collective-permute-done.1.refs_0_ = bf16[128,768]{1,0:T(8,128)(2,1)S(1)} collective-permute-done((bf16[128,768]{1,0:T(8,128)(2,1)}, bf16[128,768]{1,0:T(8,128)(2,1)S(1)}, u32[]{:S(2)}, u32[]{:S(2)}) %collective-permute-start.1) | collective-permute-done | bytes 196640 | tf_op jit(solution)/shard_map/ppermute | solution.py:428
  8.7 3.1 %collective-permute-done.2.refs_1_ = bf16[128,768]{1,0:T(8,128)(2,1)S(1)} collective-permute-done((bf16[128,768]{1,0:T(8,128)(2,1)}, bf16[128,768]{1,0:T(8,128)(2,1)S(1)}, u32[]{:S(2)}, u32[]{:S(2)}) %collective-permute-start.2) | collective-permute-done | bytes 196640 | tf_op jit(solution)/shard_map/ppermute | solution.py:429
  11.8 4.3 %shard_map.79.shared = bf16[528,768]{1,0:T(8,128)(2,1)S(1)} custom-call(bf16[128,768]{1,0:T(8,128)(2,1)S(1)} %collective-permute-done.1.refs_0_, bf16[128,768]{1,0:T(8,128)(2,1)S(1)} %collective-permute-done.2.refs_1_, bf16[1536,768]{1,0:T(8,128)(2,1)} %refs_2_.1, bf16[1536,768]{1,0:T(8,128)(2,1)} %refs_3_.1), custom_call_target="tpu_custom_call" | custom-call | flops 1207959552 | tf_op jit(solution)/shard_map/pallas_call | solution.py:142
  16.1 0.1 collective-permute-start.3
  16.2 25.3 %all_to_all.15 = bf16[64,16,128]{2,1,0:T(8,128)(2,1)S(1)} all-to-all(bf16[64,16,128]{2,1,0:T(8,128)(2,1)S(1)} %get-tuple-element.19), channel_id=1, replica_groups=mesh['y'=4,'xl'=2,'z'=8,'c'=2,'xh'=2] {'y','xl','z'}, dimensions={0} | all-to-all | bytes 524288 | tf_op jit(solution)/shard_map/all_to_all | solution.py:416
  41.5 2.2 %all_gather.3 = bf16[128,16,128]{2,1,0:T(8,128)(2,1)S(1)} all-gather(bf16[64,16,128]{2,1,0:T(8,128)(2,1)S(1)} %all_to_all.15), channel_id=1, replica_groups=mesh['y'=4,'xl'=2,'z'=8,'c'=2,'xh'=2] {'c'}, dimensions={0}, use_global_device_ids=true | all-gather | bytes 786432 | tf_op jit(solution)/shard_map/all_gather | solution.py:440
  43.7 0.0 collective-permute-done.shared_s
  43.7 4.5 %shard_map.78 = (bf16[384,512]{1,0:T(8,128)(2,1)}, bf16[512,768]{1,0:T(8,128)(2,1)}, bf16[512,768]{1,0:T(8,128)(2,1)}, bf16[384,768]{1,0:T(8,128)(2,1)}, bf16[38...) custom-call(bf16[528,768]{1,0:T(8,128)(2,1)S(1)} %get-tuple-element.20.shared, ...), custom_call_target="tpu_custom_call" | custom-call | flops 1207959552 | tf_op jit(solution)/shard_map/pallas_call | solution.py:229
  48.2 0.0 collective-permute-done.3.shared_s
  48.2 1.7 %shard_map.80 = (bf16[384,512]{1,0:T(8,128)(2,1)}, bf16[512,768]{1,0:T(8,128)(2,1)}, bf16[512,768]{1,0:T(8,128)(2,1)}, bf16[384,512]{1,0:T(8,128)(2,1)S(1)}) custom-call(bf16[528,768]{1,0:T(8,128)(2,1)S(1)} %shard_map.79.shared, bf16[528,768]{1,0:T(8,128)(2,1)S(1)} %collective-permute-done.3.shared_s, bf16[384,768]{1,0:T(8,128)(2,1)S(1)} %get-tuple-element.22.wu_mine, ...), custom_call_target="tpu_custom_call" | custom-call | flops 1207959552 | tf_op jit(solution)/shard_map/pallas_call | solution.py:260
  49.9 4.7 %shard_map.81 = (bf16[384,768]{1,0:T(8,128)(2,1)S(1)}, f32[8,128]{1,0:T(8,128)S(1)}) custom-call(bf16[2048,128]{1,0:T(8,128)(2,1)S(1)} %bitcast.7, bf16[384,512]{1,0:T(8,128)(2,1)S(1)} %get-tuple-element.21.along, bf16[384,512]{1,0:T(8,128)(2,1)S(1)} %get-tuple-element.24.along_f, bf16[384,768]{1,0:T(8,128)(2,1)} %get-tuple-element.25.wd_hbm, ...), custom_call_target="tpu_custom_call" | custom-call | tf_op jit(solution)/shard_map/pallas_call | solution.py:348
  54.6 13.9 %all_to_all.16.arrived = bf16[4,96,768]{2,1,0:T(8,128)(2,1)S(1)} all-to-all(bf16[4,96,768]{2,1,0:T(8,128)(2,1)S(1)} %bitcast.9), channel_id=1, replica_groups=mesh['y'=4,'xl'=2,'z'=8,'c'=2,'xh'=2] {'y'}, dimensions={0} | all-to-all | bytes 1179648 | tf_op jit(solution)/shard_map/all_to_all | solution.py:416
  68.5 0.2 shard_map.82
  68.7 16.6 %all_to_all.17.arrived = bf16[16,8,768]{2,1,0:T(8,128)(2,1)S(1)} all-to-all(bf16[16,8,768]{2,1,0:T(8,128)(2,1)S(1)} %bitcast.8), channel_id=1, replica_groups=mesh['y'=4,'xl'=2,'z'=8,'c'=2,'xh'=2] {'z','xh'}, dimensions={0} | all-to-all | bytes 393216 | tf_op jit(solution)/shard_map/all_to_all | solution.py:416
  85.3 0.6 shard_map.83
Async XLA Ops:
  0.6 8.1 %collective-permute-start.1 = (bf16[128,768]{1,0:T(8,128)(2,1)}, bf16[128,768]{1,0:T(8,128)(2,1)S(1)}, u32[]{:S(2)}, u32[]{:S(2)}) collective-permute-start(bf16[128,768]{1,0:T(8,128)(2,1)} %bitcast.10), channel_id=1, source_target_pairs={{0,32},{32,0},{1,33},{33,1},{2,34},{34,2},{3,35},{35,3},{4,36},{36... | collective-permute-start | bytes 589832 | tf_op jit(solution)/shard_map/ppermute | solution.py:428
  2.2 9.6 %collective-permute-start.2 = (bf16[128,768]{1,0:T(8,128)(2,1)}, bf16[128,768]{1,0:T(8,128)(2,1)S(1)}, u32[]{:S(2)}, u32[]{:S(2)}) collective-permute-start(bf16[128,768]{1,0:T(8,128)(2,1)} %bitcast.12), channel_id=1, source_target_pairs={{0,32},{32,0},{1,33},{33,1},{2,34},{34,2},{3,35},{35,3},{4,36},{36... | collective-permute-start | bytes 589832 | tf_op jit(solution)/shard_map/ppermute | solution.py:429
  7.5 36.1 %collective-permute-start = (bf16[528,768]{1,0:T(8,128)(2,1)S(1)}, bf16[528,768]{1,0:T(8,128)(2,1)S(1)}, u32[]{:S(2)}, u32[]{:S(2)}) collective-permute-start(bf16[528,768]{1,0:T(8,128)(2,1)S(1)} %get-tuple-element.20.shared), channel_id=1, source_target_pairs={{0,2},{2,0},{1,3},{3,1},{4,6},{6,4},{5,7},{7,5},{8,10},{10,8},{9,1... | collective-permute-start | bytes 2433032 | tf_op jit(solution)/shard_map/ppermute | solution.py:433
  16.1 32.1 %collective-permute-start.3 = (bf16[528,768]{1,0:T(8,128)(2,1)S(1)}, bf16[528,768]{1,0:T(8,128)(2,1)S(1)}, u32[]{:S(2)}, u32[]{:S(2)}) collective-permute-start(bf16[528,768]{1,0:T(8,128)(2,1)S(1)} %shard_map.79.shared), channel_id=1, source_target_pairs={{0,2},{2,0},{1,3},{3,1},{4,6},{6,4},{5,7},{7,5},{8,10},{10,8},{9,1... | collective-permute-start | bytes 2433032 | tf_op jit(solution)/shard_map/ppermute | solution.py:435
